TPU v7x, 32 devices: a whole 2x2x4 slice. The times are simulated.
32 devices in a mesh: dom: 8 (over y, x, core), feat: 4 (over z).
Axes of the slice: x: 2, y: 2, z: 4, core: 2. Of those that a mesh axis runs over, the one named last changes fastest.
Arguments:
- features: bfloat16 [128, 131072], P('feat', 'dom'), may hold values from -6 to 6
- seed_rows: int32 [2048], P('dom'), may hold values from 0 to 16383
- want_rows: int32 [8, 8, 128], P('dom'), may hold values from 0 to 16383
- live_counts: int32 [8, 8], P('dom'), may hold values from 1 to 128, as said below
- hop_one: int32 [15, 2048], P(None, 'dom'), may hold values from 0 to 1023, as said below
- hop_two: int32 [10, 15, 2048], P(None, None, 'dom'), may hold values from 0 to 1023, as said below
- w1_self: bfloat16 [256, 128], replicated, may hold values from -0.5 to 0.5
- w1_neigh: bfloat16 [256, 128], replicated, may hold values from -0.5 to 0.5
- b1: float32 [256], P('feat'), may hold values from -4 to 4
- w2_self: bfloat16 [256, 256], P(None, 'feat'), may hold values from -0.375 to 0.375
- w2_neigh: bfloat16 [256, 256], P(None, 'feat'), may hold values from -0.375 to 0.375
- b2: float32 [256], P('feat'), may hold values from -4 to 4
Outputs:
- embed: float32 [256, 2048], P('feat', 'dom')
Inputs may be any that keep to these rules, and one draw needn't show every extreme that they name: `want_rows`: slots at or beyond live_counts[r, o] are ignored. `live_counts`: in every draw a quarter of the owners, every fourth one from a drawn offset, receive all 128 slots from every requester. `hop_one`: each entry is o * 128 + c, a position in the buffer of the requester that holds seed s, with c < live_counts of that requester and owner o. `hop_two`: each entry is o * 128 + c, a position in the buffer of the requester that holds seed s, with c < live_counts of that requester and owner o.
All inputs are finite; a program needn't handle non-finite values.
Results may differ from a plain program's by a relative error of at most 0.00036.
Values may be sent and summed in bfloat16 or wider, within the bound.
A program may use at most 64 MiB of HBM per device.

v0:
```python
import functools

import jax
import jax.numpy as jnp
from jax import lax
from jax.experimental import pallas as pl
from jax.experimental.pallas import tpu as pltpu
from jax.sharding import PartitionSpec as P

LANES = 128
MESH = pl.DeviceIdType.MESH
BF16 = jnp.bfloat16
F32 = jnp.float32


def gather_columns(feat_vm, rows):
    height, nodes = feat_vm.shape
    shape = (height, LANES)
    high = [jnp.broadcast_to(r >> 7, shape) for r in rows]
    low = [jnp.broadcast_to(r & (LANES - 1), shape) for r in rows]
    step = min(32, nodes // LANES)

    def body(i, accs):
        for u in range(step):
            t = i * step + u
            start = pl.multiple_of(t * LANES, LANES)
            tile = feat_vm[:, pl.ds(start, LANES)].astype(F32)
            accs = tuple(
                jnp.where(
                    h == t,
                    jnp.take_along_axis(tile, l, axis=1, mode="promise_in_bounds"),
                    a,
                )
                for a, h, l in zip(accs, high, low)
            )
        return accs

    init = tuple(jnp.zeros(shape, F32) for _ in rows)
    return lax.fori_loop(0, nodes // LANES // step, body, init)


def split_three(x):
    a = x.astype(BF16)
    rest = x - a.astype(F32)
    b = rest.astype(BF16)
    c = (rest - b.astype(F32)).astype(BF16)
    return a, b, c


def kernel(
    nd,
    nf,
    feat_hbm,
    seed_ref,
    want_ref,
    live_ref,
    one_hbm,
    two_hbm,
    w1s_hbm,
    w1n_hbm,
    w2s_ref,
    w2n_ref,
    b1_ref,
    b2_ref,
    out_ref,
    feat_vm,
    one_ref,
    two_ref,
    w1s_ref,
    w1n_ref,
    got,
    served,
    back,
    everyone,
    seed_own,
    seed_all,
    w2_all,
    b1_all,
    b2_all,
    hop_rows,
    pick_one,
    pick_two,
    fetched,
    own_sum,
    mean_sum,
    x_all,
    m_all,
    w2_full,
    z_own,
    z_all,
    local_sem,
    want_send,
    want_recv,
    serve_send,
    serve_recv,
    all_send,
    all_recv,
    seed_send,
    seed_recv,
    early_send,
    early_recv,
    z_send,
    z_recv,
):
    height = feat_vm.shape[0]
    fan1, seeds = one_ref.shape
    fan2 = two_ref.shape[0]
    sub = seeds // nf
    per = LANES // sub
    chunks = (fan1 + 1) * sub // LANES
    hid_dev = out_ref.shape[0]
    hid = w1s_ref.shape[0]
    depth = w1s_ref.shape[1]
    me = lax.axis_index("dom")
    mf = lax.axis_index("feat")

    def dom_at(d):
        return lax.rem(me + d, nd)

    def feat_at(d):
        return lax.rem(mf + d, nf)

    feat_copy = pltpu.make_async_copy(feat_hbm, feat_vm, local_sem.at[0])
    feat_copy.start()
    hop_copies = [
        pltpu.make_async_copy(one_hbm, one_ref, local_sem.at[1]),
        pltpu.make_async_copy(two_hbm, two_ref, local_sem.at[2]),
    ]
    weight_copies = [
        pltpu.make_async_copy(w1s_hbm, w1s_ref, local_sem.at[3]),
        pltpu.make_async_copy(w1n_hbm, w1n_ref, local_sem.at[4]),
        pltpu.make_async_copy(w2s_ref, w2_all.at[0, mf], local_sem.at[5]),
        pltpu.make_async_copy(w2n_ref, w2_all.at[1, mf], local_sem.at[6]),
    ]

    barrier = pltpu.get_barrier_semaphore()
    for d in range(1, nd):
        pl.semaphore_signal(barrier, inc=1, device_id={"dom": dom_at(d)}, device_id_type=MESH)
    for d in range(1, nf):
        pl.semaphore_signal(barrier, inc=1, device_id={"feat": feat_at(d)}, device_id_type=MESH)
    pl.semaphore_wait(barrier, nd + nf - 2)

    def remote(src, dst, send, recv, where):
        copy = pltpu.make_async_remote_copy(
            src_ref=src,
            dst_ref=dst,
            send_sem=send,
            recv_sem=recv,
            device_id=where,
            device_id_type=MESH,
        )
        copy.start()
        return copy

    wants = [
        remote(want_ref.at[0], got.at[me], want_send.at[d], want_recv.at[d], {"dom": dom_at(d)})
        for d in range(1, nd)
    ]
    early = []
    for d in range(1, nf):
        where = {"feat": feat_at(d)}
        for i, (src, dst) in enumerate(
            (
                (b1_ref, b1_all.at[mf]),
                (b2_ref, b2_all.at[mf]),
                (w2s_ref, w2_all.at[0, mf]),
                (w2n_ref, w2_all.at[1, mf]),
            )
        ):
            early.append(remote(src, dst, early_send.at[d, i], early_recv.at[d, i], where))
    got[me] = want_ref[0]
    b1_all[mf] = b1_ref[...]
    b2_all[mf] = b2_ref[...]
    for copy in hop_copies + weight_copies:
        copy.start()

    feat_copy.wait()
    groups = seeds // LANES
    for g, block in enumerate(
        gather_columns(feat_vm, [seed_ref[:, g * LANES : (g + 1) * LANES] for g in range(groups)])
    ):
        seed_own[g] = block.astype(BF16)
    seed_copies = [
        remote(
            seed_own.at[feat_at(d) * sub // LANES],
            seed_all.at[mf],
            seed_send.at[d],
            seed_recv.at[d],
            {"feat": feat_at(d)},
        )
        for d in range(1, nf)
    ]
    seed_all[mf] = seed_own[mf * sub // LANES]

    for copy in wants:
        copy.wait_recv()

    def forward(part):
        copies = []
        for d in part:
            source = lax.rem(me + nd - d, nd)
            if d:
                serves[d].wait_recv()
            for e in range(1, nf):
                copies.append(
                    remote(
                        back.at[source],
                        everyone.at[mf, source],
                        all_send.at[d, e],
                        all_recv.at[d, e],
                        {"feat": feat_at(e)},
                    )
                )
            everyone[mf, source] = back[source]
        return copies

    serves = {}
    arrivals = []
    parts = []
    order = list(range(1, nd)) + [0]
    for part in (order[: nd * 3 // 8], order[nd * 3 // 8 : nd * 6 // 8], order[nd * 6 // 8 :]):
        blocks = gather_columns(feat_vm, [got[dom_at(d), pl.ds(me, 1), :] for d in part])
        for d, block in zip(part, blocks):
            if d == 0:
                back[me] = block.astype(BF16)
                continue
            served[d] = block.astype(BF16)
            serves[d] = remote(
                served.at[d], back.at[me], serve_send.at[d], serve_recv.at[d], {"dom": dom_at(d)}
            )
        if parts:
            arrivals.append(forward(parts[-1]))
        parts.append(part)

    lane = lax.broadcasted_iota(jnp.int32, (1, LANES), 1)
    base = pl.multiple_of(mf * sub // LANES * LANES, LANES)
    within = lax.rem(mf * sub, LANES)
    for copy in hop_copies:
        copy.wait()
    for k in range(fan2 + 1):
        if k < fan2:
            rows = two_ref[k, :, pl.ds(base, LANES)]
        else:
            rows = one_ref[:, pl.ds(base, LANES)]
        turned = [
            pltpu.roll(rows, lax.rem(q * sub - within + LANES, LANES), 1) for q in range(per)
        ]
        for c in range(chunks):
            row = jnp.full((1, LANES), -1, jnp.int32)
            for q in range(per):
                j = c * per + q
                if j < fan1:
                    inside = (lane >= q * sub) & (lane < (q + 1) * sub)
                    row = jnp.where(inside, turned[q][j : j + 1], row)
            hop_rows[c, k : k + 1, :] = row

    slot = lax.broadcasted_iota(jnp.int32, (LANES, LANES), 0)

    def build(o, carry):
        start = pl.multiple_of(o * LANES, LANES)
        place = slot + lax.rem(me + 2 * nd - 1 - o, nd) * LANES
        for c in range(chunks):
            columns = slice(c * LANES, (c + 1) * LANES)
            count = jnp.zeros((LANES, LANES), F32)
            for k in range(fan2):
                count = count + jnp.where(hop_rows[c, k : k + 1, :] == place, 1.0, 0.0)
            pick_two[pl.ds(start, LANES), columns] = count.astype(BF16)
            pick_one[pl.ds(start, LANES), columns] = jnp.where(
                hop_rows[c, fan2 : fan2 + 1, :] == place, 1.0, 0.0
            ).astype(BF16)
        return carry

    half = nd // 2
    lax.fori_loop(0, half, build, 0)

    arrivals.append(forward(parts[-1]))
    everyone_copies = [copy for part in arrivals for copy in part]

    lax.fori_loop(half, nd, build, 0)

    for copy in early:
        copy.wait_recv()
    for copy in weight_copies:
        copy.wait()
    w2_full[...] = jnp.transpose(w2_all[...].reshape(2 * hid, w2_all.shape[3]))

    def column(rows):
        return jnp.concatenate(
            [jnp.transpose(jnp.broadcast_to(rows[f], (LANES, hid_dev))) for f in range(nf)], axis=0
        )

    b1 = column(b1_all)
    b2 = column(b2_all)
    for copy in seed_copies:
        copy.wait_recv()
    if height % 16:
        x_seed = seed_all[...].astype(F32).reshape(depth, LANES)
    else:
        x_seed = seed_all[...].reshape(depth, LANES).astype(F32)
    x_seed = pltpu.roll(x_seed, lax.rem(2 * LANES - sub - within, LANES), 1)

    wide = 2 * LANES
    total = jnp.zeros((depth, LANES), F32)
    done = 0
    for i, part in enumerate(parts):
        for copy in arrivals[i]:
            copy.wait_recv()
        for d in part:
            source = lax.rem(me + nd - d, nd)
            live = lane < live_ref[0, source]
            if height % 16:
                block = everyone[:, source].astype(F32).reshape(depth, LANES)
            else:
                block = everyone[:, source].reshape(depth, LANES).astype(F32)
            at = order.index(d) * LANES
            fetched[:, at : at + LANES] = jnp.where(live, block, 0.0).astype(BF16)
        these = slice(done, done + len(part) * LANES)
        done += len(part) * LANES
        for n in range(chunks * LANES // wide):
            columns = slice(n * wide, (n + 1) * wide)
            own = jnp.dot(fetched[:, these], pick_one[these, columns], preferred_element_type=F32)
            mean = jnp.dot(fetched[:, these], pick_two[these, columns], preferred_element_type=F32)
            if i:
                own = own + own_sum[:, columns]
                mean = mean + mean_sum[:, columns]
            if i < len(parts) - 1:
                own_sum[:, columns] = own
                mean_sum[:, columns] = mean
                continue
            total = total + own[:, :LANES] + own[:, LANES:]
            x_all[:, columns] = own.astype(BF16)
            m_all[:, columns] = (mean * (1.0 / fan2)).astype(BF16)

    def fold(value):
        width = sub
        while width < LANES:
            value = value + pltpu.roll(value, width, 1)
            width *= 2
        return value

    is_seed = lane >= LANES - sub
    last = slice((chunks - 1) * LANES, chunks * LANES)
    m_one = fold(total) * (1.0 / fan1)
    x_all[:, last] = jnp.where(is_seed, x_seed, x_all[:, last].astype(F32)).astype(BF16)
    m_all[:, last] = jnp.where(is_seed, m_one, m_all[:, last].astype(F32)).astype(BF16)

    total = jnp.zeros((hid, LANES), F32)
    for n in range(chunks * LANES // wide):
        columns = slice(n * wide, (n + 1) * wide)
        pre = jnp.dot(w1s_ref[...], x_all[:, columns], preferred_element_type=F32)
        pre = pre + jnp.dot(w1n_ref[...], m_all[:, columns], preferred_element_type=F32)
        left = jnp.maximum(pre[:, :LANES] + b1, 0.0)
        right = jnp.maximum(pre[:, LANES:] + b1, 0.0)
        if n == chunks * LANES // wide - 1:
            h_seed = right
            right = jnp.where(is_seed, 0.0, right)
        total = total + left + right
    g_mean = fold(total) * (1.0 / fan1)
    stacked = jnp.concatenate([h_seed, g_mean], axis=0)
    z = jnp.zeros((hid, LANES), F32)
    for term in reversed(split_three(stacked)):
        z = z + jnp.dot(w2_full[...], term, preferred_element_type=F32)
    z = z + b2
    square = jnp.sum(z * z, axis=0, keepdims=True)
    z = z * lax.rsqrt(square * (1.0 / hid) + 1.0)
    part_rows = hid_dev // per
    for f in range(nf):
        packed = jnp.zeros((part_rows, LANES), F32)
        for p in range(per):
            row = f * hid_dev + p * part_rows
            value = z[row : row + part_rows]
            shift = (p * sub + sub) % LANES
            if shift:
                value = pltpu.roll(value, shift, 1)
            packed = jnp.where((lane >= p * sub) & (lane < (p + 1) * sub), value, packed)
        z_own[f] = packed

    z_copies = [
        remote(
            z_own.at[feat_at(d)],
            z_all.at[mf],
            z_send.at[d],
            z_recv.at[d],
            {"feat": feat_at(d)},
        )
        for d in range(1, nf)
    ]
    z_all[mf] = z_own[mf]
    for copy in wants + early + seed_copies + list(serves.values()) + everyone_copies:
        copy.wait_send()
    for copy in z_copies:
        copy.wait_recv()
    for g in range(groups):
        for p in range(per):
            block = jnp.zeros((part_rows, LANES), F32)
            for q in range(per):
                value = z_all[g * per + q]
                shift = (q - p) * sub % LANES
                if shift:
                    value = pltpu.roll(value, shift, 1)
                inside = (lane >= q * sub) & (lane < (q + 1) * sub)
                block = jnp.where(inside, value, block)
            out_ref[p * part_rows : (p + 1) * part_rows, g * LANES : (g + 1) * LANES] = block
    for copy in z_copies:
        copy.wait_send()


def per_device(
    nd,
    nf,
    features,
    seed_rows,
    want_rows,
    live_counts,
    hop_one,
    hop_two,
    w1_self,
    w1_neigh,
    b1,
    w2_self,
    w2_neigh,
    b2,
):
    height, nodes = features.shape
    seeds = seed_rows.shape[0]
    hid_dev = b1.shape[0]
    hid, depth = w1_self.shape
    cap = want_rows.shape[2]
    fan1 = hop_one.shape[0]
    fan2 = hop_two.shape[0]
    columns = (fan1 + 1) * (seeds // nf)
    vmem = pl.BlockSpec(memory_space=pltpu.VMEM)
    dma = pltpu.SemaphoreType.DMA
    return pl.pallas_call(
        functools.partial(kernel, nd, nf),
        out_shape=pltpu.VMEM((hid_dev, seeds), F32),
        in_specs=[
            pl.BlockSpec(memory_space=pl.ANY),
            vmem,
            vmem,
            pl.BlockSpec(memory_space=pltpu.SMEM),
        ]
        + [pl.BlockSpec(memory_space=pl.ANY)] * 6
        + [vmem] * 2,
        out_specs=vmem,
        scratch_shapes=[
            pltpu.VMEM((height, nodes), BF16),
            pltpu.VMEM(hop_one.shape, jnp.int32),
            pltpu.VMEM(hop_two.shape, jnp.int32),
            pltpu.VMEM(w1_self.shape, BF16),
            pltpu.VMEM(w1_neigh.shape, BF16),
            pltpu.VMEM((nd, nd, cap), jnp.int32),
            pltpu.VMEM((nd, height, cap), BF16),
            pltpu.VMEM((nd, height, cap), BF16),
            pltpu.VMEM((nf, nd, height, cap), BF16),
            pltpu.VMEM((seeds // LANES, height, LANES), BF16),
            pltpu.VMEM((nf, height, LANES), BF16),
            pltpu.VMEM((2, nf, hid_dev, w2_self.shape[0]), BF16),
            pltpu.VMEM((nf, 1, hid_dev), F32),
            pltpu.VMEM((nf, 1, hid_dev), F32),
            pltpu.VMEM((columns // LANES, 16, LANES), jnp.int32),
            pltpu.VMEM((nd * cap, columns), BF16),
            pltpu.VMEM((nd * cap, columns), BF16),
            pltpu.VMEM((depth, nd * cap), BF16),
            pltpu.VMEM((depth, columns), F32),
            pltpu.VMEM((depth, columns), F32),
            pltpu.VMEM((depth, columns), BF16),
            pltpu.VMEM((depth, columns), BF16),
            pltpu.VMEM((hid, 2 * hid), BF16),
            pltpu.VMEM((nf, hid_dev * (seeds // nf) // LANES, LANES), F32),
            pltpu.VMEM((nf, hid_dev * (seeds // nf) // LANES, LANES), F32),
            dma((7,)),
        ]
        + [dma((nd,))] * 4
        + [dma((nd, nf))] * 2
        + [dma((nf,))] * 2
        + [dma((nf, 4))] * 2
        + [dma((nf,))] * 2,
        compiler_params=pltpu.CompilerParams(collective_id=0, has_side_effects=True),
    )(
        features,
        seed_rows.reshape(1, seeds),
        want_rows,
        live_counts,
        hop_one,
        hop_two,
        w1_self,
        w1_neigh,
        w2_self.T,
        w2_neigh.T,
        b1.reshape(1, hid_dev),
        b2.reshape(1, hid_dev),
    )


def solution(mesh):
    return jax.shard_map(
        functools.partial(per_device, mesh.shape["dom"], mesh.shape["feat"]),
        mesh=mesh,
        in_specs=(
            P("feat", "dom"),
            P("dom"),
            P("dom", None, None),
            P("dom", None),
            P(None, "dom"),
            P(None, None, "dom"),
            P(),
            P(),
            P("feat"),
            P(None, "feat"),
            P(None, "feat"),
            P("feat"),
        ),
        out_specs=P("feat", "dom"),
        check_vma=False,
    )
```

profile of v0, /device:TPU:0, one launch (start us, length us, event | category | flops | bytes accessed | tf_op | source)
XLA Modules:
  0.0 30.0 jit_solution(2480106891857820166)
XLA Ops:
  0.0 29.3 %shard_map.118 = f32[64,256]{1,0:T(8,128)S(1)} custom-call(bf16[32,16384]{1,0:T(8,128)(2,1)} %feat_hbm.1, s32[1,256]{1,0:T(1,128)} %bitcast.7, s32[1,8,128]{2,1,0:T(8,128)} %want_ref.1, s32[1,8]{1,0:T(1,128)} %live_ref.1, s32[15,256]{1,0:T(8,128)} %one_hbm.1, s32[10,15,256]{2,1,0:T(8,128)} %two_hbm.1, bf16[256,128]{1,0:T(8,128)(2,1)} %w1s_hbm.1, ...), custom_call_target="tpu_custom_call" | custom-call | tf_op jit(solution)/shard_map/pallas_call | solution.py:434
  29.3 0.6 %copy.14 = f32[64,256]{1,0:T(8,128)} copy(f32[64,256]{1,0:T(8,128)S(1)} %shard_map.118) | data formatting | bytes 131072
where the time goes:
time: 30.2 us; the launch traced here: 30 us
  Pallas kernels  29.3 us (97%)
  local copies, waits for them, and re-layouts  0.63 us (2%)
    pallas_call x1, Pallas kernels, per_device(): pl.pallas_call(functools.partial(kernel, nd, nf), out_shape=pltpu.VMEM((h...  29.3 us
    unnamed x1, local copies, waits for them, and re-layouts  0.63 us

commit v1 on v0

v1 whole, which is shorter than its diff:
```python
import functools

import jax
import jax.numpy as jnp
from jax import lax
from jax.experimental import pallas as pl
from jax.experimental.pallas import tpu as pltpu
from jax.sharding import PartitionSpec as P

LANES = 128
MESH = pl.DeviceIdType.MESH
BF16 = jnp.bfloat16
F32 = jnp.float32


def split_three(x):
    a = x.astype(BF16)
    rest = x - a.astype(F32)
    b = rest.astype(BF16)
    c = (rest - b.astype(F32)).astype(BF16)
    return a, b, c


def kernel(
    nd,
    nf,
    feat_hbm,
    seed_hbm,
    want_hbm,
    live_hbm,
    one_hbm,
    two_hbm,
    w1s_hbm,
    w1n_hbm,
    w2s_hbm,
    w2n_hbm,
    b1_hbm,
    b2_hbm,
    out_ref,
    feat_vm,
    seed_vm,
    seed_sm,
    want_vm,
    live_sm,
    one_ref,
    two_ref,
    w1s_ref,
    w1n_ref,
    ask,
    got,
    got_sm,
    table,
    rows_vm,
    served,
    everyone,
    seed_own,
    seed_all,
    w2_all,
    b1_all,
    b2_all,
    hop_rows,
    words,
    pick_one,
    pick_two,
    own_sum,
    mean_sum,
    x_all,
    m_all,
    w2_full,
    z_own,
    z_all,
    local_sem,
    ready,
    want_send,
    want_recv,
    want_sm_send,
    want_sm_recv,
    data_send,
    data_recv,
    seed_send,
    seed_recv,
    early_send,
    early_recv,
    z_send,
    z_recv,
):
    height, nodes = feat_vm.shape
    fan1, seeds = one_ref.shape
    fan2 = two_ref.shape[0]
    sub = seeds // nf
    per = LANES // sub
    chunks = (fan1 + 1) * sub // LANES
    hid_dev = out_ref.shape[0]
    hid = w1s_ref.shape[0]
    depth = w1s_ref.shape[1]
    groups = seeds // LANES
    pieces = depth // height
    table_rows = nodes // pieces
    me = lax.axis_index("dom")
    mf = lax.axis_index("feat")

    def dom_at(d):
        return lax.rem(me + d, nd)

    def feat_at(d):
        return lax.rem(mf + d, nf)

    def local(i, src, dst):
        copy = pltpu.make_async_copy(src, dst, local_sem.at[i])
        copy.start()
        return copy

    barrier = pltpu.get_barrier_semaphore()
    for d in range(1, nf):
        pl.semaphore_signal(barrier, inc=1, device_id={"feat": feat_at(d)}, device_id_type=MESH)
    for d in range(1, nd):
        pl.semaphore_signal(barrier, inc=1, device_id={"dom": dom_at(d)}, device_id_type=MESH)

    want_copies = [local(0, want_hbm.at[0], want_vm), local(1, live_hbm, live_sm)]
    feat_copy = local(2, feat_hbm, feat_vm)
    early_copies = [
        local(3, w2s_hbm, w2_all.at[0, mf]),
        local(4, w2n_hbm, w2_all.at[1, mf]),
        local(5, b1_hbm, b1_all.at[mf]),
        local(6, b2_hbm, b2_all.at[mf]),
    ]
    seed_local = [local(7, seed_hbm, seed_vm), local(8, seed_hbm, seed_sm)]
    hop_copies = [local(9, one_hbm, one_ref), local(10, two_hbm, two_ref)]
    weight_copies = [local(11, w1s_hbm, w1s_ref), local(12, w1n_hbm, w1n_ref)]

    def remote(src, dst, send, recv, where):
        copy = pltpu.make_async_remote_copy(
            src_ref=src,
            dst_ref=dst,
            send_sem=send,
            recv_sem=recv,
            device_id=where,
            device_id_type=MESH,
        )
        copy.start()
        return copy

    lane = lax.broadcasted_iota(jnp.int32, (1, LANES), 1)
    for copy in want_copies:
        copy.wait()
    for o in range(nd):
        ask[o] = jnp.where(lane < live_sm[0, o], want_vm[o : o + 1], -1)
    pl.semaphore_wait(barrier, nd + nf - 2)

    wants = []
    for d in range(1, nd):
        pl.semaphore_signal(ready, inc=1, device_id={"dom": dom_at(d)}, device_id_type=MESH)
    for d in range(1, nd):
        where = {"dom": dom_at(d)}
        src = ask.at[dom_at(d)]
        wants.append(remote(src, got_sm.at[d], want_sm_send.at[d], want_sm_recv.at[d], where))
        wants.append(remote(src, got.at[d], want_send.at[d], want_recv.at[d], where))
    own_sm = local(13, ask.at[me], got_sm.at[0])
    got[0] = ask[me]
    for copy in early_copies:
        copy.wait()
    early = []
    for d in range(1, nf):
        where = {"feat": feat_at(d)}
        for i, ref in enumerate(
            (b1_all.at[mf], b2_all.at[mf], w2_all.at[0, mf], w2_all.at[1, mf])
        ):
            early.append(remote(ref, ref, early_send.at[d, i], early_recv.at[d, i], where))

    feat_copy.wait()
    tiles = table_rows // LANES
    step = min(8, tiles)

    def turn(i, carry):
        for u in range(step):
            t = i * step + u
            stack = jnp.concatenate(
                [
                    feat_vm[
                        :, pl.ds(pl.multiple_of(p * table_rows + t * LANES, LANES), LANES)
                    ].astype(F32)
                    for p in range(pieces)
                ],
                axis=0,
            )
            table[pl.ds(pl.multiple_of(t * LANES, LANES), LANES), :] = jnp.transpose(stack)
        return carry

    lax.fori_loop(0, tiles // step, turn, 0)

    def gather(slot, read, wanted):
        burst = 32

        def body(i, carry):
            for u in range(burst):
                k = i * burst + u
                row = read(k) & (table_rows - 1)
                rows_vm[slot, pl.ds(k, 1), :] = table[pl.ds(row, 1), :]
            return carry

        lax.fori_loop(0, LANES // burst, body, 0)
        turned = jnp.transpose(rows_vm[slot])
        piece = wanted >> (table_rows.bit_length() - 1)
        block = jnp.zeros((height, LANES), F32)
        for p in range(pieces):
            block = jnp.where(piece == p, turned[p * height : (p + 1) * height], block)
        return block.astype(BF16)

    for copy in seed_local:
        copy.wait()
    for g in range(groups):
        seed_own[g] = gather(
            nd + g,
            lambda k: seed_sm[0, g * LANES + k],
            seed_vm[:, g * LANES : (g + 1) * LANES],
        )
    seed_copies = [
        remote(
            seed_own.at[feat_at(d) * sub // LANES],
            seed_all.at[mf],
            seed_send.at[d],
            seed_recv.at[d],
            {"feat": feat_at(d)},
        )
        for d in range(1, nf)
    ]
    seed_all[mf] = seed_own[mf * sub // LANES]

    order = list(range(1, nd)) + [0]
    parts = [order[: nd * 3 // 8], order[nd * 3 // 8 : nd * 6 // 8], order[nd * 6 // 8 :]]
    data = {}
    pl.semaphore_wait(ready, nd - 1)
    for d in order:
        if d:
            wants[2 * d - 2].wait_recv()
            wants[2 * d - 1].wait_recv()
        else:
            own_sm.wait()
        served[d] = gather(d, lambda k: got_sm[d, 0, k], got[d])
        for e in range(nf - 1, -1, -1):
            where = {"dom": dom_at(nd - d), "feat": feat_at(e)}
            if d or e:
                data[d, e] = remote(
                    served.at[d],
                    everyone.at[d, mf],
                    data_send.at[d, e],
                    data_recv.at[d, e],
                    where,
                )
        if d == 0:
            everyone[0, mf] = served[0]

    base = pl.multiple_of(mf * sub // LANES * LANES, LANES)
    within = lax.rem(mf * sub, LANES)
    for copy in hop_copies:
        copy.wait()
    for k in range(fan2 + 1):
        if k < fan2:
            rows = two_ref[k, :, pl.ds(base, LANES)]
        else:
            rows = one_ref[:, pl.ds(base, LANES)]
        rel = (rows >> 7) - me - 1
        rows = (rows & (LANES - 1)) + jnp.where(rel < 0, rel + nd, rel) * LANES
        turned = [
            pltpu.roll(rows, lax.rem(q * sub - within + LANES, LANES), 1) for q in range(per)
        ]
        for c in range(chunks):
            row = jnp.full((1, LANES), -1, jnp.int32)
            for q in range(per):
                j = c * per + q
                if j < fan1:
                    inside = (lane >= q * sub) & (lane < (q + 1) * sub)
                    row = jnp.where(inside, turned[q][j : j + 1], row)
            hop_rows[c, k : k + 1, :] = row

    slot = lax.broadcasted_iota(jnp.int32, (LANES, LANES), 0)
    each = 8
    for c in range(chunks):
        columns = slice(c * LANES, (c + 1) * LANES)
        for g in range(words.shape[0]):
            count = jnp.zeros((LANES, LANES), jnp.int32)
            for k in range(fan2):
                row = hop_rows[c, k : k + 1, :]
                rel = (row >> 7) - g * each
                real = (row >= 0) & (rel >= 0) & (rel < each)
                unit = jnp.where(real, jnp.left_shift(1, (rel & (each - 1)) * 4), 0)
                count = count + jnp.where((row & (LANES - 1)) == slot, unit, 0)
            words[g, :, columns] = count

    def build(o, carry):
        start = pl.multiple_of(o * LANES, LANES)
        place = slot + o * LANES
        shift = lax.rem(o, each) * 4
        for c in range(chunks):
            columns = slice(c * LANES, (c + 1) * LANES)
            count = lax.shift_right_logical(words[o // each, :, columns], shift) & 15
            pick_two[pl.ds(start, LANES), columns] = count.astype(F32).astype(BF16)
            pick_one[pl.ds(start, LANES), columns] = jnp.where(
                hop_rows[c, fan2 : fan2 + 1, :] == place, 1.0, 0.0
            ).astype(BF16)
        return carry

    lax.fori_loop(0, nd, build, 0)

    for copy in early:
        copy.wait_recv()
    for copy in weight_copies:
        copy.wait()
    w2_full[...] = jnp.transpose(w2_all[...].reshape(2 * hid, w2_all.shape[3]))

    def column(rows):
        return jnp.concatenate(
            [jnp.transpose(jnp.broadcast_to(rows[f], (LANES, hid_dev))) for f in range(nf)], axis=0
        )

    b1 = column(b1_all)
    b2 = column(b2_all)
    for copy in seed_copies:
        copy.wait_recv()

    def whole(blocks):
        if height % 16:
            return blocks.astype(F32).reshape(depth, LANES).astype(BF16)
        return blocks.reshape(depth, LANES)

    x_seed = whole(seed_all[...]).astype(F32)
    x_seed = pltpu.roll(x_seed, lax.rem(2 * LANES - sub - within, LANES), 1)

    wide = 2 * LANES
    total = jnp.zeros((depth, LANES), F32)
    done = 0
    for i, part in enumerate(parts):
        for d in part:
            for e in range(nf):
                if d or e:
                    data[d, e].wait_recv()
        fetched = jnp.concatenate([whole(everyone[d]) for d in part], axis=1)
        these = slice(done, done + len(part) * LANES)
        done += len(part) * LANES
        for n in range(chunks * LANES // wide):
            columns = slice(n * wide, (n + 1) * wide)
            own = jnp.dot(fetched, pick_one[these, columns], preferred_element_type=F32)
            mean = jnp.dot(fetched, pick_two[these, columns], preferred_element_type=F32)
            if i:
                own = own + own_sum[:, columns]
                mean = mean + mean_sum[:, columns]
            if i < len(parts) - 1:
                own_sum[:, columns] = own
                mean_sum[:, columns] = mean
                continue
            total = total + own[:, :LANES] + own[:, LANES:]
            x_all[:, columns] = own.astype(BF16)
            m_all[:, columns] = (mean * (1.0 / fan2)).astype(BF16)

    def fold(value):
        width = sub
        while width < LANES:
            value = value + pltpu.roll(value, width, 1)
            width *= 2
        return value

    is_seed = lane >= LANES - sub
    last = slice((chunks - 1) * LANES, chunks * LANES)
    m_one = fold(total) * (1.0 / fan1)
    x_all[:, last] = jnp.where(is_seed, x_seed, x_all[:, last].astype(F32)).astype(BF16)
    m_all[:, last] = jnp.where(is_seed, m_one, m_all[:, last].astype(F32)).astype(BF16)

    total = jnp.zeros((hid, LANES), F32)
    for n in range(chunks * LANES // wide):
        columns = slice(n * wide, (n + 1) * wide)
        pre = jnp.dot(w1s_ref[...], x_all[:, columns], preferred_element_type=F32)
        pre = pre + jnp.dot(w1n_ref[...], m_all[:, columns], preferred_element_type=F32)
        left = jnp.maximum(pre[:, :LANES] + b1, 0.0)
        right = jnp.maximum(pre[:, LANES:] + b1, 0.0)
        if n == chunks * LANES // wide - 1:
            h_seed = right
            right = jnp.where(is_seed, 0.0, right)
        total = total + left + right
    g_mean = fold(total) * (1.0 / fan1)
    stacked = jnp.concatenate([h_seed, g_mean], axis=0)
    z = jnp.zeros((hid, LANES), F32)
    for term in reversed(split_three(stacked)):
        z = z + jnp.dot(w2_full[...], term, preferred_element_type=F32)
    z = z + b2
    square = jnp.sum(z * z, axis=0, keepdims=True)
    z = z * lax.rsqrt(square * (1.0 / hid) + 1.0)
    part_rows = hid_dev // per
    for f in range(nf):
        packed = jnp.zeros((part_rows, LANES), F32)
        for p in range(per):
            row = f * hid_dev + p * part_rows
            value = z[row : row + part_rows]
            shift = (p * sub + sub) % LANES
            if shift:
                value = pltpu.roll(value, shift, 1)
            packed = jnp.where((lane >= p * sub) & (lane < (p + 1) * sub), value, packed)
        z_own[f] = packed

    z_copies = [
        remote(
            z_own.at[feat_at(d)],
            z_all.at[mf],
            z_send.at[d],
            z_recv.at[d],
            {"feat": feat_at(d)},
        )
        for d in range(1, nf)
    ]
    z_all[mf] = z_own[mf]
    for copy in wants + early + seed_copies + list(data.values()):
        copy.wait_send()
    for copy in z_copies:
        copy.wait_recv()
    for g in range(groups):
        for p in range(per):
            block = jnp.zeros((part_rows, LANES), F32)
            for q in range(per):
                value = z_all[g * per + q]
                shift = (q - p) * sub % LANES
                if shift:
                    value = pltpu.roll(value, shift, 1)
                inside = (lane >= q * sub) & (lane < (q + 1) * sub)
                block = jnp.where(inside, value, block)
            out_ref[p * part_rows : (p + 1) * part_rows, g * LANES : (g + 1) * LANES] = block
    for copy in z_copies:
        copy.wait_send()


def per_device(
    nd,
    nf,
    features,
    seed_rows,
    want_rows,
    live_counts,
    hop_one,
    hop_two,
    w1_self,
    w1_neigh,
    b1,
    w2_self,
    w2_neigh,
    b2,
):
    height, nodes = features.shape
    seeds = seed_rows.shape[0]
    hid_dev = b1.shape[0]
    hid, depth = w1_self.shape
    cap = want_rows.shape[2]
    fan1 = hop_one.shape[0]
    columns = (fan1 + 1) * (seeds // nf)
    groups = seeds // LANES
    vmem = pl.BlockSpec(memory_space=pltpu.VMEM)
    dma = pltpu.SemaphoreType.DMA
    return pl.pallas_call(
        functools.partial(kernel, nd, nf),
        out_shape=pltpu.VMEM((hid_dev, seeds), F32),
        in_specs=[pl.BlockSpec(memory_space=pl.ANY)] * 12,
        out_specs=vmem,
        scratch_shapes=[
            pltpu.VMEM((height, nodes), BF16),
            pltpu.VMEM((1, seeds), jnp.int32),
            pltpu.SMEM((1, seeds), jnp.int32),
            pltpu.VMEM((nd, cap), jnp.int32),
            pltpu.SMEM((1, nd), jnp.int32),
            pltpu.VMEM(hop_one.shape, jnp.int32),
            pltpu.VMEM(hop_two.shape, jnp.int32),
            pltpu.VMEM(w1_self.shape, BF16),
            pltpu.VMEM(w1_neigh.shape, BF16),
            pltpu.VMEM((nd, 1, cap), jnp.int32),
            pltpu.VMEM((nd, 1, cap), jnp.int32),
            pltpu.SMEM((nd, 1, cap), jnp.int32),
            pltpu.VMEM((nodes * height // depth, LANES), F32),
            pltpu.VMEM((nd + groups, LANES, LANES), F32),
            pltpu.VMEM((nd, height, cap), BF16),
            pltpu.VMEM((nd, nf, height, cap), BF16),
            pltpu.VMEM((groups, height, LANES), BF16),
            pltpu.VMEM((nf, height, LANES), BF16),
            pltpu.VMEM((2, nf, hid_dev, w2_self.shape[0]), BF16),
            pltpu.VMEM((nf, 1, hid_dev), F32),
            pltpu.VMEM((nf, 1, hid_dev), F32),
            pltpu.VMEM((columns // LANES, 16, LANES), jnp.int32),
            pltpu.VMEM((pl.cdiv(nd, 8), LANES, columns), jnp.int32),
            pltpu.VMEM((nd * cap, columns), BF16),
            pltpu.VMEM((nd * cap, columns), BF16),
            pltpu.VMEM((depth, columns), F32),
            pltpu.VMEM((depth, columns), F32),
            pltpu.VMEM((depth, columns), BF16),
            pltpu.VMEM((depth, columns), BF16),
            pltpu.VMEM((hid, 2 * hid), BF16),
            pltpu.VMEM((nf, hid_dev * (seeds // nf) // LANES, LANES), F32),
            pltpu.VMEM((nf, hid_dev * (seeds // nf) // LANES, LANES), F32),
            dma((14,)),
            pltpu.SemaphoreType.REGULAR,
        ]
        + [dma((nd,))] * 4
        + [dma((nd, nf))] * 2
        + [dma((nf,))] * 2
        + [dma((nf, 4))] * 2
        + [dma((nf,))] * 2,
        compiler_params=pltpu.CompilerParams(collective_id=0, has_side_effects=True),
    )(
        features,
        seed_rows.reshape(1, seeds),
        want_rows,
        live_counts,
        hop_one,
        hop_two,
        w1_self,
        w1_neigh,
        w2_self.T,
        w2_neigh.T,
        b1.reshape(1, hid_dev),
        b2.reshape(1, hid_dev),
    )


def solution(mesh):
    return jax.shard_map(
        functools.partial(per_device, mesh.shape["dom"], mesh.shape["feat"]),
        mesh=mesh,
        in_specs=(
            P("feat", "dom"),
            P("dom"),
            P("dom", None, None),
            P("dom", None),
            P(None, "dom"),
            P(None, None, "dom"),
            P(),
            P(),
            P("feat"),
            P(None, "feat"),
            P(None, "feat"),
            P("feat"),
        ),
        out_specs=P("feat", "dom"),
        check_vma=False,
    )
```

time: 30.2 us -> 27.5 us (0.911)
  Pallas kernels: 29.3 us -> 26.7 us
    pallas_call x1, Pallas kernels: 29.3 us -> 26.7 us  [per_device(): pl.pallas_call(functools.partial(kernel, nd, nf), out_shape=pltpu.VMEM((h...]
where the time goes in v1:
time: 27.5 us; the launch traced here: 27.3 us
  Pallas kernels  26.7 us (97%)
  local copies, waits for them, and re-layouts  0.63 us (2%)
    pallas_call x1, Pallas kernels, per_device(): pl.pallas_call(functools.partial(kernel, nd, nf), out_shape=pltpu.VMEM((h...  26.7 us
    unnamed x1, local copies, waits for them, and re-layouts  0.63 us

profile of v1, /device:TPU:0, one launch (start us, length us, event | category | flops | bytes accessed | tf_op | source)
XLA Modules:
  0.0 27.3 jit_solution(13643833688322237468)
XLA Ops:
  0.0 26.7 %shard_map.118 = f32[64,256]{1,0:T(8,128)S(1)} custom-call(bf16[32,16384]{1,0:T(8,128)(2,1)} %feat_hbm.1, s32[1,256]{1,0:T(1,128)} %bitcast.7, s32[1,8,128]{2,1,0:T(8,128)} %want_hbm.1, s32[1,8]{1,0:T(1,128)} %live_hbm.1, s32[15,256]{1,0:T(8,128)} %one_hbm.1, s32[10,15,256]{2,1,0:T(8,128)} %two_hbm.1, bf16[256,128]{1,0:T(8,128)(2,1)} %w1s_hbm.1, ...), custom_call_target="tpu_custom_call" | custom-call | tf_op jit(solution)/shard_map/pallas_call | solution.py:455
  26.7 0.6 %copy.14 = f32[64,256]{1,0:T(8,128)} copy(f32[64,256]{1,0:T(8,128)S(1)} %shard_map.118) | data formatting | bytes 131072

commit v2 on v1

--- a/solution.py
+++ b/solution.py
@@ -81,12 +81,16 @@
     seed_recv,
     early_send,
     early_recv,
+    pair_send,
+    pair_recv,
+    pass_send,
+    pass_recv,
     z_send,
     z_recv,
 ):
     height, nodes = feat_vm.shape
-    fan1, seeds = one_ref.shape
-    fan2 = two_ref.shape[0]
+    _, fan1, seeds = one_ref.shape
+    fan2 = two_ref.shape[1]
     sub = seeds // nf
     per = LANES // sub
     chunks = (fan1 + 1) * sub // LANES
@@ -98,9 +102,26 @@
     table_rows = nodes // pieces
     me = lax.axis_index("dom")
     mf = lax.axis_index("feat")
-
-    def dom_at(d):
-        return lax.rem(me + d, nd)
+    pairs = nd // 2
+    half = nf // 2
+    odd = lax.rem(me, 2)
+    late = mf // half
+    home = odd == late
+    worker = odd * half + lax.rem(mf, half)
+
+    def flip(x, bits):
+        bit = 1
+        while bit <= bits:
+            if bits & bit:
+                x = x + bit * (1 - 2 * lax.rem(x // bit, 2))
+            bit *= 2
+        return x
+
+    def other(t):
+        return odd + t * (1 - 2 * odd)
+
+    def dom_at(d, t):
+        return 2 * flip(me // 2, d) + other(t)
 
     def feat_at(d):
         return lax.rem(mf + d, nf)
@@ -113,8 +134,9 @@
     barrier = pltpu.get_barrier_semaphore()
     for d in range(1, nf):
         pl.semaphore_signal(barrier, inc=1, device_id={"feat": feat_at(d)}, device_id_type=MESH)
-    for d in range(1, nd):
-        pl.semaphore_signal(barrier, inc=1, device_id={"dom": dom_at(d)}, device_id_type=MESH)
+    peers = [(d, t) for d in range(pairs) for t in range(2)][1:]
+    for d, t in peers:
+        pl.semaphore_signal(barrier, inc=1, device_id={"dom": dom_at(d, t)}, device_id_type=MESH)
 
     want_copies = [local(0, want_hbm.at[0], want_vm), local(1, live_hbm, live_sm)]
     feat_copy = local(2, feat_hbm, feat_vm)
@@ -125,7 +147,7 @@
         local(6, b2_hbm, b2_all.at[mf]),
     ]
     seed_local = [local(7, seed_hbm, seed_vm), local(8, seed_hbm, seed_sm)]
-    hop_copies = [local(9, one_hbm, one_ref), local(10, two_hbm, two_ref)]
+    hop_copies = [local(9, one_hbm, one_ref.at[0]), local(10, two_hbm, two_ref.at[0])]
     weight_copies = [local(11, w1s_hbm, w1s_ref), local(12, w1n_hbm, w1n_ref)]
 
     def remote(src, dst, send, recv, where):
@@ -147,25 +169,30 @@
         ask[o] = jnp.where(lane < live_sm[0, o], want_vm[o : o + 1], -1)
     pl.semaphore_wait(barrier, nd + nf - 2)
 
-    wants = []
-    for d in range(1, nd):
-        pl.semaphore_signal(ready, inc=1, device_id={"dom": dom_at(d)}, device_id_type=MESH)
-    for d in range(1, nd):
-        where = {"dom": dom_at(d)}
-        src = ask.at[dom_at(d)]
-        wants.append(remote(src, got_sm.at[d], want_sm_send.at[d], want_sm_recv.at[d], where))
-        wants.append(remote(src, got.at[d], want_send.at[d], want_recv.at[d], where))
-    own_sm = local(13, ask.at[me], got_sm.at[0])
-    got[0] = ask[me]
+    for d, t in peers:
+        pl.semaphore_signal(ready, inc=1, device_id={"dom": dom_at(d, t)}, device_id_type=MESH)
+    wants = {}
+    for d, t in peers:
+        where = {"dom": dom_at(d, t)}
+        src = ask.at[dom_at(d, t)]
+        wants[d, t] = [
+            remote(src, got_sm.at[d, t], want_sm_send.at[d, t], want_sm_recv.at[d, t], where),
+            remote(src, got.at[d, t], want_send.at[d, t], want_recv.at[d, t], where),
+        ]
+    own_sm = local(13, ask.at[me], got_sm.at[0, 0])
+    got[0, 0] = ask[me]
     for copy in early_copies:
         copy.wait()
+    buddy = {"dom": dom_at(0, 1)}
     early = []
     for d in range(1, nf):
         where = {"feat": feat_at(d)}
-        for i, ref in enumerate(
-            (b1_all.at[mf], b2_all.at[mf], w2_all.at[0, mf], w2_all.at[1, mf])
-        ):
+        for i, ref in enumerate((b1_all.at[mf], b2_all.at[mf], w2_all.at[odd, mf])):
             early.append(remote(ref, ref, early_send.at[d, i], early_recv.at[d, i], where))
+    hops = [
+        remote(one_hbm, one_ref.at[1], pair_send.at[0], pair_recv.at[0], buddy),
+        remote(two_hbm, two_ref.at[1], pair_send.at[1], pair_recv.at[1], buddy),
+    ]
 
     feat_copy.wait()
     tiles = table_rows // LANES
@@ -214,53 +241,87 @@
             lambda k: seed_sm[0, g * LANES + k],
             seed_vm[:, g * LANES : (g + 1) * LANES],
         )
-    seed_copies = [
-        remote(
-            seed_own.at[feat_at(d) * sub // LANES],
-            seed_all.at[mf],
-            seed_send.at[d],
-            seed_recv.at[d],
-            {"feat": feat_at(d)},
-        )
-        for d in range(1, nf)
-    ]
-    seed_all[mf] = seed_own[mf * sub // LANES]
-
-    order = list(range(1, nd)) + [0]
-    parts = [order[: nd * 3 // 8], order[nd * 3 // 8 : nd * 6 // 8], order[nd * 6 // 8 :]]
+    own_feat = jnp.logical_not(home)
+    seed_copies = []
+    for t in range(2):
+        for i in range(half):
+            to = odd * half + lax.rem(mf + i, half)
+            which = other(t) * half + lax.rem(mf + i, half)
+            copy = pltpu.make_async_remote_copy(
+                src_ref=seed_own.at[which * sub // LANES],
+                dst_ref=seed_all.at[mf],
+                send_sem=seed_send.at[t, i],
+                recv_sem=seed_recv.at[mf],
+                device_id={"dom": dom_at(0, t), "feat": to},
+                device_id_type=MESH,
+            )
+            seed_copies.append(copy)
+
+    pl.semaphore_wait(ready, nd - 1)
+    for n, copy in enumerate(seed_copies):
+        if n == 0:
+            pl.when(own_feat)(copy.start)
+        else:
+            copy.start()
+
+    @pl.when(home)
+    def _():
+        seed_all[mf] = seed_own[worker * sub // LANES]
+
     data = {}
-    pl.semaphore_wait(ready, nd - 1)
-    for d in order:
-        if d:
-            wants[2 * d - 2].wait_recv()
-            wants[2 * d - 1].wait_recv()
-        else:
-            own_sm.wait()
-        served[d] = gather(d, lambda k: got_sm[d, 0, k], got[d])
-        for e in range(nf - 1, -1, -1):
-            where = {"dom": dom_at(nd - d), "feat": feat_at(e)}
-            if d or e:
-                data[d, e] = remote(
-                    served.at[d],
-                    everyone.at[d, mf],
-                    data_send.at[d, e],
-                    data_recv.at[d, e],
-                    where,
+    for d in range(pairs):
+        for t in range(2):
+            if d or t:
+                for copy in wants[d, t]:
+                    copy.wait_recv()
+            else:
+                own_sm.wait()
+            served[d, t] = gather(2 * d + t, lambda k: got_sm[d, t, 0, k], got[d, t])
+            for e in range(half if d else 0):
+                data[d, t, e] = remote(
+                    served.at[d, t],
+                    everyone.at[0, d, mf],
+                    data_send.at[d, t * half + e],
+                    data_recv.at[d, mf],
+                    {"dom": dom_at(d, 0), "feat": other(t) * half + e},
                 )
         if d == 0:
-            everyone[0, mf] = served[0]
-
-    base = pl.multiple_of(mf * sub // LANES * LANES, LANES)
-    within = lax.rem(mf * sub, LANES)
+            for e in range(1, nf):
+                to = feat_at(e)
+                data[0, 0, e] = remote(
+                    served.at[0, lax.rem(to // half + odd, 2)],
+                    everyone.at[0, 0, mf],
+                    data_send.at[0, e],
+                    data_recv.at[0, mf],
+                    {"feat": to},
+                )
+            everyone[0, 0, mf] = served[0, lax.rem(late + odd, 2)]
+
+    def arrived(d):
+        for f in range(nf):
+            for_me = pltpu.make_async_copy(
+                everyone.at[0, d, f], everyone.at[0, d, f], data_recv.at[d, f]
+            )
+            if d:
+                for_me.wait()
+            else:
+                pl.when(mf != f)(for_me.wait)
+
+    base = pl.multiple_of(worker * sub // LANES * LANES, LANES)
+    within = lax.rem(worker * sub, LANES)
     for copy in hop_copies:
         copy.wait()
+    for copy in hops:
+        copy.wait_recv()
+    mine = lax.rem(odd + late, 2)
     for k in range(fan2 + 1):
         if k < fan2:
-            rows = two_ref[k, :, pl.ds(base, LANES)]
+            rows = two_ref[mine, k, :, pl.ds(base, LANES)]
         else:
-            rows = one_ref[:, pl.ds(base, LANES)]
-        rel = (rows >> 7) - me - 1
-        rows = (rows & (LANES - 1)) + jnp.where(rel < 0, rel + nd, rel) * LANES
+            rows = one_ref[mine, :, pl.ds(base, LANES)]
+        owner = rows >> 7
+        rel = ((owner >> 1) ^ (me // 2)) + ((owner & 1) ^ odd) * pairs
+        rows = (rows & (LANES - 1)) + rel * LANES
         turned = [
             pltpu.roll(rows, lax.rem(q * sub - within + LANES, LANES), 1) for q in range(per)
         ]
@@ -304,8 +365,24 @@
 
     for copy in early:
         copy.wait_recv()
+    swaps = []
+    for d in range(1, nf):
+        ref = w2_all.at[odd, feat_at(d)]
+        swaps.append(remote(ref, ref, pair_send.at[1 + d], pair_recv.at[1 + d], buddy))
+    forwards = []
+
+    def forward(d):
+        arrived(d)
+        forwards.append(
+            remote(everyone.at[0, d], everyone.at[1, d], pass_send.at[d], pass_recv.at[d], buddy)
+        )
+
+    for d in range(pairs):
+        forward(d)
     for copy in weight_copies:
         copy.wait()
+    for copy in swaps:
+        copy.wait_recv()
     w2_full[...] = jnp.transpose(w2_all[...].reshape(2 * hid, w2_all.shape[3]))
 
     def column(rows):
@@ -315,8 +392,9 @@
 
     b1 = column(b1_all)
     b2 = column(b2_all)
-    for copy in seed_copies:
-        copy.wait_recv()
+    for f in range(nf):
+        for_me = pltpu.make_async_copy(seed_all.at[f], seed_all.at[f], seed_recv.at[f])
+        pl.when(jnp.logical_not(home & (mf == f)))(for_me.wait)
 
     def whole(blocks):
         if height % 16:
@@ -329,12 +407,13 @@
     wide = 2 * LANES
     total = jnp.zeros((depth, LANES), F32)
     done = 0
+    order = [(t, d) for t in range(2) for d in range(pairs)]
+    parts = [order[:pairs], order[pairs:]]
     for i, part in enumerate(parts):
-        for d in part:
-            for e in range(nf):
-                if d or e:
-                    data[d, e].wait_recv()
-        fetched = jnp.concatenate([whole(everyone[d]) for d in part], axis=1)
+        if i:
+            for copy in forwards:
+                copy.wait_recv()
+        fetched = jnp.concatenate([whole(everyone[t, d]) for t, d in part], axis=1)
         these = slice(done, done + len(part) * LANES)
         done += len(part) * LANES
         for n in range(chunks * LANES // wide):
@@ -396,21 +475,34 @@
             packed = jnp.where((lane >= p * sub) & (lane < (p + 1) * sub), value, packed)
         z_own[f] = packed
 
-    z_copies = [
-        remote(
-            z_own.at[feat_at(d)],
-            z_all.at[mf],
-            z_send.at[d],
-            z_recv.at[d],
-            {"feat": feat_at(d)},
+    z_copies = []
+    for e in range(nf):
+        to = feat_at(e)
+        copy = pltpu.make_async_remote_copy(
+            src_ref=z_own.at[to],
+            dst_ref=z_all.at[worker],
+            send_sem=z_send.at[e],
+            recv_sem=z_recv.at[worker],
+            device_id={"dom": 2 * (me // 2) + late, "feat": to},
+            device_id_type=MESH,
         )
-        for d in range(1, nf)
-    ]
-    z_all[mf] = z_own[mf]
-    for copy in wants + early + seed_copies + list(data.values()):
+        z_copies.append(copy)
+        if e:
+            copy.start()
+        else:
+            pl.when(own_feat)(copy.start)
+
+    @pl.when(home)
+    def _():
+        z_all[worker] = z_own[mf]
+
+    pl.when(own_feat)(seed_copies[0].wait_send)
+    sent = early + hops + swaps + forwards + seed_copies[1:] + list(data.values())
+    for copy in sent + [copy for both in wants.values() for copy in both]:
         copy.wait_send()
-    for copy in z_copies:
-        copy.wait_recv()
+    for w in range(nf):
+        for_me = pltpu.make_async_copy(z_all.at[w], z_all.at[w], z_recv.at[w])
+        pl.when(jnp.logical_not(home & (worker == w)))(for_me.wait)
     for g in range(groups):
         for p in range(per):
             block = jnp.zeros((part_rows, LANES), F32)
@@ -422,7 +514,8 @@
                 inside = (lane >= q * sub) & (lane < (q + 1) * sub)
                 block = jnp.where(inside, value, block)
             out_ref[p * part_rows : (p + 1) * part_rows, g * LANES : (g + 1) * LANES] = block
-    for copy in z_copies:
+    pl.when(own_feat)(z_copies[0].wait_send)
+    for copy in z_copies[1:]:
         copy.wait_send()
 
 
@@ -463,17 +556,17 @@
             pltpu.SMEM((1, seeds), jnp.int32),
             pltpu.VMEM((nd, cap), jnp.int32),
             pltpu.SMEM((1, nd), jnp.int32),
-            pltpu.VMEM(hop_one.shape, jnp.int32),
-            pltpu.VMEM(hop_two.shape, jnp.int32),
+            pltpu.VMEM((2,) + hop_one.shape, jnp.int32),
+            pltpu.VMEM((2,) + hop_two.shape, jnp.int32),
             pltpu.VMEM(w1_self.shape, BF16),
             pltpu.VMEM(w1_neigh.shape, BF16),
             pltpu.VMEM((nd, 1, cap), jnp.int32),
-            pltpu.VMEM((nd, 1, cap), jnp.int32),
-            pltpu.SMEM((nd, 1, cap), jnp.int32),
+            pltpu.VMEM((nd // 2, 2, 1, cap), jnp.int32),
+            pltpu.SMEM((nd // 2, 2, 1, cap), jnp.int32),
             pltpu.VMEM((nodes * height // depth, LANES), F32),
             pltpu.VMEM((nd + groups, LANES, LANES), F32),
-            pltpu.VMEM((nd, height, cap), BF16),
-            pltpu.VMEM((nd, nf, height, cap), BF16),
+            pltpu.VMEM((nd // 2, 2, height, cap), BF16),
+            pltpu.VMEM((2, nd // 2, nf, height, cap), BF16),
             pltpu.VMEM((groups, height, LANES), BF16),
             pltpu.VMEM((nf, height, LANES), BF16),
             pltpu.VMEM((2, nf, hid_dev, w2_self.shape[0]), BF16),
@@ -493,10 +586,12 @@
             dma((14,)),
             pltpu.SemaphoreType.REGULAR,
         ]
-        + [dma((nd,))] * 4
-        + [dma((nd, nf))] * 2
-        + [dma((nf,))] * 2
-        + [dma((nf, 4))] * 2
+        + [dma((nd // 2, 2))] * 4
+        + [dma((nd // 2, nf))] * 2
+        + [dma((2, nf // 2)), dma((nf,))]
+        + [dma((nf, 3))] * 2
+        + [dma((nf + 1,))] * 2
+        + [dma((nd // 2,))] * 2
         + [dma((nf,))] * 2,
         compiler_params=pltpu.CompilerParams(collective_id=0, has_side_effects=True),
     )(

time: 27.5 us -> 22.8 us (0.83)
  the two profiles are of different devices: /device:TPU:0 before, /device:TPU:1 now
where the time goes in v2:
time: 22.8 us; the launch traced here: 22.6 us
  Pallas kernels  22 us (96%)
  local copies, waits for them, and re-layouts  0.63 us (3%)
    pallas_call x1, Pallas kernels, per_device(): pl.pallas_call(functools.partial(kernel, nd, nf), out_shape=pltpu.VMEM((h...  22 us
    unnamed x1, local copies, waits for them, and re-layouts  0.63 us

profile of v2, /device:TPU:1, one launch (start us, length us, event | category | flops | bytes accessed | tf_op | source)
XLA Modules:
  0.0 22.6 jit_solution(14476613771023341763)
XLA Ops:
  0.0 22.0 %shard_map.118 = f32[64,256]{1,0:T(8,128)S(1)} custom-call(bf16[32,16384]{1,0:T(8,128)(2,1)} %feat_hbm.1, s32[1,256]{1,0:T(1,128)} %bitcast.7, s32[1,8,128]{2,1,0:T(8,128)} %want_hbm.1, s32[1,8]{1,0:T(1,128)} %live_hbm.1, s32[15,256]{1,0:T(8,128)} %one_hbm.1, s32[10,15,256]{2,1,0:T(8,128)} %two_hbm.1, bf16[256,128]{1,0:T(8,128)(2,1)} %w1s_hbm.1, ...), custom_call_target="tpu_custom_call" | custom-call | tf_op jit(solution)/shard_map/pallas_call | solution.py:548
  22.0 0.6 %copy.14 = f32[64,256]{1,0:T(8,128)} copy(f32[64,256]{1,0:T(8,128)S(1)} %shard_map.118) | data formatting | bytes 131072

commit v3 on v1

v3 whole, which is shorter than its diff:
```python
import functools

import jax
import jax.numpy as jnp
from jax import lax
from jax.experimental import pallas as pl
from jax.experimental.pallas import tpu as pltpu
from jax.sharding import PartitionSpec as P

LANES = 128
MESH = pl.DeviceIdType.MESH
BF16 = jnp.bfloat16
F32 = jnp.float32


def split_three(x):
    a = x.astype(BF16)
    rest = x - a.astype(F32)
    b = rest.astype(BF16)
    c = (rest - b.astype(F32)).astype(BF16)
    return a, b, c


def kernel(
    nd,
    nf,
    feat_hbm,
    seed_hbm,
    want_hbm,
    live_hbm,
    one_hbm,
    two_hbm,
    w1s_hbm,
    w1n_hbm,
    w2s_hbm,
    w2n_hbm,
    b1_hbm,
    b2_hbm,
    out_ref,
    feat_vm,
    seed_vm,
    seed_sm,
    want_vm,
    live_sm,
    one_ref,
    two_ref,
    w1_ref,
    ask,
    ask_row,
    got,
    got_sm,
    table,
    rows_vm,
    served,
    everyone,
    seed_own,
    seed_all,
    w2_all,
    b1_all,
    b2_all,
    hop_rows,
    words,
    pick_one,
    pick_two,
    own_sum,
    mean_sum,
    xm_all,
    w2_full,
    z_own,
    z_all,
    local_sem,
    ready,
    want_send,
    want_recv,
    want_sm_send,
    want_sm_recv,
    data_send,
    data_recv,
    seed_send,
    seed_recv,
    early_send,
    early_recv,
    pair_send,
    pair_recv,
    z_send,
    z_recv,
):
    height, nodes = feat_vm.shape
    fan1, seeds = one_ref.shape
    fan2 = two_ref.shape[0]
    workers = nf // 2
    first = nf // 4
    sub = seeds // workers
    per = LANES // sub
    chunks = (fan1 + 1) * sub // LANES
    hid_dev = out_ref.shape[0]
    hid = w1_ref.shape[0]
    depth = w1_ref.shape[1] // 2
    part_rows = hid_dev // per
    groups = seeds // LANES
    pieces = depth // height
    table_rows = nodes // pieces
    me = lax.axis_index("dom")
    mf = lax.axis_index("feat")
    pairs = nd // 2
    odd = lax.rem(me, 2)
    mine = mf - first
    works = (mf >= first) & (mf < first + workers)

    def flip(x, bits):
        bit = 1
        while bit <= bits:
            if bits & bit:
                x = x + bit * (1 - 2 * lax.rem(x // bit, 2))
            bit *= 2
        return x

    def other(t):
        return odd + t * (1 - 2 * odd)

    def dom_at(d, t):
        return 2 * flip(me // 2, d) + other(t)

    def feat_at(d):
        return lax.rem(mf + d, nf)

    def local(i, src, dst):
        copy = pltpu.make_async_copy(src, dst, local_sem.at[i])
        copy.start()
        return copy

    barrier = pltpu.get_barrier_semaphore()
    for d in range(1, nf):
        pl.semaphore_signal(barrier, inc=1, device_id={"feat": feat_at(d)}, device_id_type=MESH)
    peers = [(d, t) for d in range(pairs) for t in range(2)][1:]
    for d, t in peers:
        pl.semaphore_signal(barrier, inc=1, device_id={"dom": dom_at(d, t)}, device_id_type=MESH)

    want_copies = [local(0, want_hbm.at[0], want_vm), local(1, live_hbm, live_sm)]
    feat_copy = local(2, feat_hbm, feat_vm)
    early_copies = [
        local(3, w2s_hbm, w2_all.at[0, mf]),
        local(4, w2n_hbm, w2_all.at[1, mf]),
        local(5, b1_hbm, b1_all.at[mf]),
        local(6, b2_hbm, b2_all.at[mf]),
    ]
    seed_local = [local(7, seed_hbm, seed_vm), local(8, seed_hbm, seed_sm)]
    hop_copies = [
        pltpu.make_async_copy(one_hbm, one_ref, local_sem.at[9]),
        pltpu.make_async_copy(two_hbm, two_ref, local_sem.at[10]),
    ]
    weight_copies = [
        pltpu.make_async_copy(w1s_hbm, w1_ref.at[:, :depth], local_sem.at[11]),
        pltpu.make_async_copy(w1n_hbm, w1_ref.at[:, depth:], local_sem.at[12]),
    ]

    @pl.when(works)
    def _():
        for copy in hop_copies + weight_copies:
            copy.start()

    def remote(src, dst, send, recv, where):
        copy = pltpu.make_async_remote_copy(
            src_ref=src,
            dst_ref=dst,
            send_sem=send,
            recv_sem=recv,
            device_id=where,
            device_id_type=MESH,
        )
        copy.start()
        return copy

    lane = lax.broadcasted_iota(jnp.int32, (1, LANES), 1)
    for copy in want_copies:
        copy.wait()
    for o in range(nd):
        wanted = jnp.where(lane < live_sm[0, o], want_vm[o : o + 1], -1)
        ask[o] = wanted
        ask_row[o] = wanted & (table_rows - 1)
    pl.semaphore_wait(barrier, nd + nf - 2)

    for d, t in peers:
        pl.semaphore_signal(ready, inc=1, device_id={"dom": dom_at(d, t)}, device_id_type=MESH)
    wants = {}
    for d, t in peers:
        where = {"dom": dom_at(d, t)}
        to = dom_at(d, t)
        sem = want_sm_send.at[d, t], want_sm_recv.at[d, t]
        wants[d, t] = [
            remote(ask_row.at[to], got_sm.at[d, t], *sem, where),
            remote(ask.at[to], got.at[d, t], want_send.at[d, t], want_recv.at[d, t], where),
        ]
    own_sm = local(13, ask_row.at[me], got_sm.at[0, 0])
    got[0, 0] = ask[me]
    for copy in early_copies:
        copy.wait()
    buddy = {"dom": dom_at(0, 1)}

    def to_worker(w, src, dst, send, recv, where):
        copy = pltpu.make_async_remote_copy(
            src_ref=src,
            dst_ref=dst,
            send_sem=send,
            recv_sem=recv,
            device_id={**where, "feat": first + w},
            device_id_type=MESH,
        )
        pl.when(mf != first + w)(copy.start)
        loose.append((w, copy))

    def landed(ref, sem, f):
        copy = pltpu.make_async_copy(ref, ref, sem)
        pl.when(mf != f)(copy.wait)

    loose = []
    for w in range(workers):
        for i, ref in enumerate((b1_all.at[mf], b2_all.at[mf], w2_all.at[odd, mf])):
            to_worker(w, ref, ref, early_send.at[w, i], early_recv.at[mf, i], {})

    feat_copy.wait()
    tiles = table_rows // LANES
    step = min(8, tiles)

    def turn(i, carry):
        for u in range(step):
            t = i * step + u
            stack = jnp.concatenate(
                [
                    feat_vm[
                        :, pl.ds(pl.multiple_of(p * table_rows + t * LANES, LANES), LANES)
                    ].astype(F32)
                    for p in range(pieces)
                ],
                axis=0,
            )
            table[pl.ds(pl.multiple_of(t * LANES, LANES), LANES), :] = jnp.transpose(stack)
        return carry

    lax.fori_loop(0, tiles // step, turn, 0)

    def gather(jobs):
        for slot, read, _ in jobs:
            for k in range(LANES):
                rows_vm[slot, k : k + 1, :] = table[pl.ds(read(k), 1), :]
        blocks = []
        for slot, _, wanted in jobs:
            turned = jnp.transpose(rows_vm[slot])
            piece = wanted >> (table_rows.bit_length() - 1)
            block = jnp.zeros((height, LANES), F32)
            for p in range(pieces):
                block = jnp.where(piece == p, turned[p * height : (p + 1) * height], block)
            blocks.append(block.astype(BF16))
        return blocks

    for copy in seed_local:
        copy.wait()
    def seed_job(g):
        at = g * LANES
        return (
            nd + g,
            lambda k: seed_sm[0, at + k] & (table_rows - 1),
            seed_vm[:, at : at + LANES],
        )

    for g, block in enumerate(gather([seed_job(g) for g in range(groups)])):
        seed_own[g] = block
    for w in range(workers):
        block = seed_own.at[w * sub // LANES]
        to_worker(w, block, seed_all.at[mf], seed_send.at[w], seed_recv.at[mf], {})

    @pl.when(works)
    def _():
        seed_all[mf] = seed_own[mine * sub // LANES]

    pl.semaphore_wait(ready, nd - 1)
    base = pl.multiple_of(mine * sub // LANES * LANES, LANES)
    within = lax.rem(mine * sub, LANES)
    slot = lax.broadcasted_iota(jnp.int32, (LANES, LANES), 0)
    each = 8
    picked = chunks if per > 1 else chunks - 1

    def prepare():
        for copy in hop_copies:
            copy.wait()
        for k in range(fan2 + 1):
            if k < fan2:
                rows = two_ref[k, :, pl.ds(base, LANES)]
            else:
                rows = one_ref[:, pl.ds(base, LANES)]
            owner = rows >> 7
            rel = ((owner >> 1) ^ (me // 2)) * 2 + ((owner & 1) ^ odd)
            rows = (rows & (LANES - 1)) + rel * LANES
            turned = [
                pltpu.roll(rows, lax.rem(q * sub - within + LANES, LANES), 1) for q in range(per)
            ]
            for c in range(chunks):
                row = jnp.full((1, LANES), -1, jnp.int32)
                for q in range(per):
                    j = c * per + q
                    if j < fan1:
                        inside = (lane >= q * sub) & (lane < (q + 1) * sub)
                        row = jnp.where(inside, turned[q][j : j + 1], row)
                hop_rows[c, k : k + 1, :] = row

        for c in range(picked):
            columns = slice(c * LANES, (c + 1) * LANES)
            for g in range(words.shape[0]):
                count = jnp.zeros((LANES, LANES), jnp.int32)
                for k in range(fan2):
                    row = hop_rows[c, k : k + 1, :]
                    rel = (row >> 7) - g * each
                    real = (row >= 0) & (rel >= 0) & (rel < each)
                    unit = jnp.where(real, jnp.left_shift(1, (rel & (each - 1)) * 4), 0)
                    count = count + jnp.where((row & (LANES - 1)) == slot, unit, 0)
                words[g, :, columns] = count

    @pl.when(works)
    def _():
        prepare()

    def work():
        def expand(owners):
            for o in owners:
                place = slot + o * LANES
                these = slice(o * LANES, (o + 1) * LANES)
                for c in range(picked):
                    columns = slice(c * LANES, (c + 1) * LANES)
                    count = lax.shift_right_logical(words[o // each, :, columns], o % each * 4)
                    pick_two[these, columns] = (count & 15).astype(F32).astype(BF16)
                    pick_one[these, columns] = jnp.where(
                        hop_rows[c, fan2 : fan2 + 1, :] == place, 1.0, 0.0
                    ).astype(BF16)

        steps = min(4, pairs)
        ends = [nd * i // steps for i in range(steps + 1)]
        expand(range(ends[0], ends[1]))
        for f in range(nf):
            for i, ref in enumerate((b1_all.at[f], b2_all.at[f], w2_all.at[odd, f])):
                landed(ref, early_recv.at[f, i], f)
        swaps = []
        for d in range(1, nf):
            ref = w2_all.at[odd, feat_at(d)]
            swaps.append(remote(ref, ref, pair_send.at[d], pair_recv.at[d], buddy))
        for copy in weight_copies:
            copy.wait()
        for copy in swaps:
            copy.wait_recv()
        w2_full[...] = jnp.transpose(w2_all[...].reshape(2 * hid, w2_all.shape[3]))

        def column(rows):
            return jnp.concatenate(
                [jnp.transpose(jnp.broadcast_to(rows[f], (LANES, hid_dev))) for f in range(nf)], axis=0
            )

        b1 = column(b1_all)
        b2 = column(b2_all)
        for f in range(nf):
            landed(seed_all.at[f], seed_recv.at[f], f)

        def whole(blocks):
            if height % 16:
                return blocks.astype(F32).reshape(depth, LANES).astype(BF16)
            return blocks.reshape(depth, LANES)

        x_seed = whole(seed_all[...]).astype(F32)
        if per > 1:
            x_seed = pltpu.roll(x_seed, lax.rem(2 * LANES - sub - within, LANES), 1)

        wide = 2 * LANES
        total = jnp.zeros((depth, LANES), F32)
        done = 0
        for i in range(steps):
            part = [(o // 2, o % 2) for o in range(ends[i], ends[i + 1])]
            if i + 1 < steps:
                expand(range(ends[i + 1], ends[i + 2]))
            for d, t in part:
                for f in range(nf):
                    if d or t:
                        spot = everyone.at[d, t, f]
                        pltpu.make_async_copy(spot, spot, data_recv.at[d, t, f]).wait()
                    else:
                        landed(everyone.at[0, 0, f], data_recv.at[0, 0, f], f)
            fetched = jnp.concatenate([whole(everyone[d, t]) for d, t in part], axis=1)
            these = slice(done, done + len(part) * LANES)
            done += len(part) * LANES
            for n in range(0, picked, 2):
                columns = slice(n * LANES, min(n + 2, picked) * LANES)
                own = jnp.dot(fetched, pick_one[these, columns], preferred_element_type=F32)
                mean = jnp.dot(fetched, pick_two[these, columns], preferred_element_type=F32)
                if i:
                    own = own + own_sum[:, columns]
                    mean = mean + mean_sum[:, columns]
                if i < steps - 1:
                    own_sum[:, columns] = own
                    mean_sum[:, columns] = mean
                    continue
                for at in range(0, own.shape[1], LANES):
                    total = total + own[:, at : at + LANES]
                xm_all[:depth, columns] = own.astype(BF16)
                xm_all[depth:, columns] = (mean * (1.0 / fan2)).astype(BF16)

        def fold(value):
            width = sub
            while width < LANES:
                value = value + pltpu.roll(value, width, 1)
                width *= 2
            return value

        is_seed = lane >= LANES - sub
        last = slice((chunks - 1) * LANES, chunks * LANES)
        m_one = fold(total) * (1.0 / fan1)
        if per > 1:
            x_seed = jnp.where(is_seed, x_seed, xm_all[:depth, last].astype(F32))
            m_one = jnp.where(is_seed, m_one, xm_all[depth:, last].astype(F32))
        xm_all[:depth, last] = x_seed.astype(BF16)
        xm_all[depth:, last] = m_one.astype(BF16)

        total = jnp.zeros((hid, LANES), F32)
        for n in range(chunks * LANES // wide):
            columns = slice(n * wide, (n + 1) * wide)
            pre = jnp.dot(w1_ref[...], xm_all[:, columns], preferred_element_type=F32)
            left = jnp.maximum(pre[:, :LANES] + b1, 0.0)
            right = jnp.maximum(pre[:, LANES:] + b1, 0.0)
            if n == chunks * LANES // wide - 1:
                h_seed = right
                right = jnp.where(is_seed, 0.0, right)
            total = total + left + right
        g_mean = fold(total) * (1.0 / fan1)
        stacked = jnp.concatenate([h_seed, g_mean], axis=0)
        z = jnp.zeros((hid, LANES), F32)
        for term in reversed(split_three(stacked)):
            z = z + jnp.dot(w2_full[...], term, preferred_element_type=F32)
        z = z + b2
        square = jnp.sum(z * z, axis=0, keepdims=True)
        z = z * lax.rsqrt(square * (1.0 / hid) + 1.0)
        for f in range(nf):
            packed = jnp.zeros((part_rows, LANES), F32)
            for p in range(per):
                row = f * hid_dev + p * part_rows
                value = z[row : row + part_rows]
                shift = (p * sub + sub) % LANES
                if shift:
                    value = pltpu.roll(value, shift, 1)
                packed = jnp.where((lane >= p * sub) & (lane < (p + 1) * sub), value, packed)
            z_own[f] = packed

        z_copies = []
        for e in range(1, nf):
            to = feat_at(e)
            where = {"feat": to}
            z_copies.append(remote(z_own.at[to], z_all.at[mine], z_send.at[e], z_recv.at[mine], where))
        z_all[mine] = z_own[mf]
        for copy in swaps + z_copies:
            copy.wait_send()

    data = []
    def want_job(d, t):
        return (2 * d + t, lambda k: got_sm[d, t, 0, k], got[d, t])

    for d in range(pairs):
        for t in range(2):
            if d or t:
                for copy in wants[d, t]:
                    copy.wait_recv()
            else:
                own_sm.wait()
        for t, block in enumerate(gather([want_job(d, t) for t in range(2)])):
            served[d, t] = block
            for w in range(workers):
                block = served.at[d, t]
                spot = everyone.at[d, t, mf]
                send = data_send.at[d, t, w]
                recv = data_recv.at[d, t, mf]
                if d or t:
                    where = {"dom": dom_at(d, t), "feat": first + w}
                    data.append(remote(block, spot, send, recv, where))
                else:
                    to_worker(w, block, spot, send, recv, {})
    everyone[0, 0, mf] = served[0, 0]

    @pl.when(works)
    def _():
        work()

    for w, copy in loose:
        pl.when(mf != first + w)(copy.wait_send)
    for copy in data + [copy for both in wants.values() for copy in both]:
        copy.wait_send()
    for w in range(workers):
        landed(z_all.at[w], z_recv.at[w], first + w)
    for g in range(groups):
        for p in range(per):
            block = jnp.zeros((part_rows, LANES), F32)
            for q in range(per):
                value = z_all[g * per + q]
                shift = (q - p) * sub % LANES
                if shift:
                    value = pltpu.roll(value, shift, 1)
                inside = (lane >= q * sub) & (lane < (q + 1) * sub)
                block = jnp.where(inside, value, block)
            out_ref[p * part_rows : (p + 1) * part_rows, g * LANES : (g + 1) * LANES] = block

def per_device(
    nd,
    nf,
    features,
    seed_rows,
    want_rows,
    live_counts,
    hop_one,
    hop_two,
    w1_self,
    w1_neigh,
    b1,
    w2_self,
    w2_neigh,
    b2,
):
    height, nodes = features.shape
    seeds = seed_rows.shape[0]
    hid_dev = b1.shape[0]
    hid, depth = w1_self.shape
    cap = want_rows.shape[2]
    fan1 = hop_one.shape[0]
    workers = nf // 2
    columns = (fan1 + 1) * (seeds // workers)
    result = (hid_dev * (seeds // workers) // LANES, LANES)
    groups = seeds // LANES
    vmem = pl.BlockSpec(memory_space=pltpu.VMEM)
    dma = pltpu.SemaphoreType.DMA
    return pl.pallas_call(
        functools.partial(kernel, nd, nf),
        out_shape=pltpu.VMEM((hid_dev, seeds), F32),
        in_specs=[pl.BlockSpec(memory_space=pl.ANY)] * 12,
        out_specs=vmem,
        scratch_shapes=[
            pltpu.VMEM((height, nodes), BF16),
            pltpu.VMEM((1, seeds), jnp.int32),
            pltpu.SMEM((1, seeds), jnp.int32),
            pltpu.VMEM((nd, cap), jnp.int32),
            pltpu.SMEM((1, nd), jnp.int32),
            pltpu.VMEM(hop_one.shape, jnp.int32),
            pltpu.VMEM(hop_two.shape, jnp.int32),
            pltpu.VMEM((hid, 2 * depth), BF16),
            pltpu.VMEM((nd, 1, cap), jnp.int32),
            pltpu.VMEM((nd, 1, cap), jnp.int32),
            pltpu.VMEM((nd // 2, 2, 1, cap), jnp.int32),
            pltpu.SMEM((nd // 2, 2, 1, cap), jnp.int32),
            pltpu.VMEM((nodes * height // depth, LANES), F32),
            pltpu.VMEM((nd + groups, LANES, LANES), F32),
            pltpu.VMEM((nd // 2, 2, height, cap), BF16),
            pltpu.VMEM((nd // 2, 2, nf, height, cap), BF16),
            pltpu.VMEM((groups, height, LANES), BF16),
            pltpu.VMEM((nf, height, LANES), BF16),
            pltpu.VMEM((2, nf, hid_dev, w2_self.shape[0]), BF16),
            pltpu.VMEM((nf, 1, hid_dev), F32),
            pltpu.VMEM((nf, 1, hid_dev), F32),
            pltpu.VMEM((columns // LANES, 16, LANES), jnp.int32),
            pltpu.VMEM((pl.cdiv(nd, 8), LANES, columns), jnp.int32),
            pltpu.VMEM((nd * cap, columns), BF16),
            pltpu.VMEM((nd * cap, columns), BF16),
            pltpu.VMEM((depth, columns), F32),
            pltpu.VMEM((depth, columns), F32),
            pltpu.VMEM((2 * depth, columns), BF16),
            pltpu.VMEM((hid, 2 * hid), BF16),
            pltpu.VMEM((nf,) + result, F32),
            pltpu.VMEM((workers,) + result, F32),
            dma((14,)),
            pltpu.SemaphoreType.REGULAR,
        ]
        + [dma((nd // 2, 2))] * 4
        + [dma((nd // 2, 2, workers)), dma((nd // 2, 2, nf))]
        + [dma((workers,)), dma((nf,))]
        + [dma((workers, 3)), dma((nf, 3))]
        + [dma((nf,))] * 2
        + [dma((nf,)), dma((workers,))],
        compiler_params=pltpu.CompilerParams(collective_id=0, has_side_effects=True),
    )(
        features,
        seed_rows.reshape(1, seeds),
        want_rows,
        live_counts,
        hop_one,
        hop_two,
        w1_self,
        w1_neigh,
        w2_self.T,
        w2_neigh.T,
        b1.reshape(1, hid_dev),
        b2.reshape(1, hid_dev),
    )


def solution(mesh):
    return jax.shard_map(
        functools.partial(per_device, mesh.shape["dom"], mesh.shape["feat"]),
        mesh=mesh,
        in_specs=(
            P("feat", "dom"),
            P("dom"),
            P("dom", None, None),
            P("dom", None),
            P(None, "dom"),
            P(None, None, "dom"),
            P(),
            P(),
            P("feat"),
            P(None, "feat"),
            P(None, "feat"),
            P("feat"),
        ),
        out_specs=P("feat", "dom"),
        check_vma=False,
    )
```

time: 27.5 us -> 21.9 us (0.80)
  Pallas kernels: 26.7 us -> 21.1 us
    pallas_call x1, Pallas kernels: 26.7 us -> 21.1 us  [per_device(): pl.pallas_call(functools.partial(kernel, nd, nf), out_shape=pltpu.VMEM((h...]
where the time goes in v3:
time: 21.9 us; the launch traced here: 21.7 us
  Pallas kernels  21.1 us (96%)
  local copies, waits for them, and re-layouts  0.63 us (3%)
    pallas_call x1, Pallas kernels, per_device(): pl.pallas_call(functools.partial(kernel, nd, nf), out_shape=pltpu.VMEM((h...  21.1 us
    unnamed x1, local copies, waits for them, and re-layouts  0.63 us

profile of v3, /device:TPU:0, one launch (start us, length us, event | category | flops | bytes accessed | tf_op | source)
XLA Modules:
  0.0 21.7 jit_solution(15070134526646555980)
XLA Ops:
  0.0 21.1 %shard_map.118 = f32[64,256]{1,0:T(8,128)S(1)} custom-call(bf16[32,16384]{1,0:T(8,128)(2,1)} %feat_hbm.1, s32[1,256]{1,0:T(1,128)} %bitcast.7, s32[1,8,128]{2,1,0:T(8,128)} %want_hbm.1, s32[1,8]{1,0:T(1,128)} %live_hbm.1, s32[15,256]{1,0:T(8,128)} %one_hbm.1, s32[10,15,256]{2,1,0:T(8,128)} %two_hbm.1, bf16[256,128]{1,0:T(8,128)(2,1)} %w1s_hbm.1, ...), custom_call_target="tpu_custom_call" | custom-call | tf_op jit(solution)/shard_map/pallas_call | solution.py:532
  21.1 0.6 %copy.14 = f32[64,256]{1,0:T(8,128)} copy(f32[64,256]{1,0:T(8,128)S(1)} %shard_map.118) | data formatting | bytes 131072

commit v4 on v3

--- a/solution.py
+++ b/solution.py
@@ -178,46 +178,6 @@
         wanted = jnp.where(lane < live_sm[0, o], want_vm[o : o + 1], -1)
         ask[o] = wanted
         ask_row[o] = wanted & (table_rows - 1)
-    pl.semaphore_wait(barrier, nd + nf - 2)
-
-    for d, t in peers:
-        pl.semaphore_signal(ready, inc=1, device_id={"dom": dom_at(d, t)}, device_id_type=MESH)
-    wants = {}
-    for d, t in peers:
-        where = {"dom": dom_at(d, t)}
-        to = dom_at(d, t)
-        sem = want_sm_send.at[d, t], want_sm_recv.at[d, t]
-        wants[d, t] = [
-            remote(ask_row.at[to], got_sm.at[d, t], *sem, where),
-            remote(ask.at[to], got.at[d, t], want_send.at[d, t], want_recv.at[d, t], where),
-        ]
-    own_sm = local(13, ask_row.at[me], got_sm.at[0, 0])
-    got[0, 0] = ask[me]
-    for copy in early_copies:
-        copy.wait()
-    buddy = {"dom": dom_at(0, 1)}
-
-    def to_worker(w, src, dst, send, recv, where):
-        copy = pltpu.make_async_remote_copy(
-            src_ref=src,
-            dst_ref=dst,
-            send_sem=send,
-            recv_sem=recv,
-            device_id={**where, "feat": first + w},
-            device_id_type=MESH,
-        )
-        pl.when(mf != first + w)(copy.start)
-        loose.append((w, copy))
-
-    def landed(ref, sem, f):
-        copy = pltpu.make_async_copy(ref, ref, sem)
-        pl.when(mf != f)(copy.wait)
-
-    loose = []
-    for w in range(workers):
-        for i, ref in enumerate((b1_all.at[mf], b2_all.at[mf], w2_all.at[odd, mf])):
-            to_worker(w, ref, ref, early_send.at[w, i], early_recv.at[mf, i], {})
-
     feat_copy.wait()
     tiles = table_rows // LANES
     step = min(8, tiles)
@@ -239,48 +199,14 @@
 
     lax.fori_loop(0, tiles // step, turn, 0)
 
-    def gather(jobs):
-        for slot, read, _ in jobs:
-            for k in range(LANES):
-                rows_vm[slot, k : k + 1, :] = table[pl.ds(read(k), 1), :]
-        blocks = []
-        for slot, _, wanted in jobs:
-            turned = jnp.transpose(rows_vm[slot])
-            piece = wanted >> (table_rows.bit_length() - 1)
-            block = jnp.zeros((height, LANES), F32)
-            for p in range(pieces):
-                block = jnp.where(piece == p, turned[p * height : (p + 1) * height], block)
-            blocks.append(block.astype(BF16))
-        return blocks
-
-    for copy in seed_local:
-        copy.wait()
-    def seed_job(g):
-        at = g * LANES
-        return (
-            nd + g,
-            lambda k: seed_sm[0, at + k] & (table_rows - 1),
-            seed_vm[:, at : at + LANES],
-        )
-
-    for g, block in enumerate(gather([seed_job(g) for g in range(groups)])):
-        seed_own[g] = block
-    for w in range(workers):
-        block = seed_own.at[w * sub // LANES]
-        to_worker(w, block, seed_all.at[mf], seed_send.at[w], seed_recv.at[mf], {})
-
-    @pl.when(works)
-    def _():
-        seed_all[mf] = seed_own[mine * sub // LANES]
-
-    pl.semaphore_wait(ready, nd - 1)
     base = pl.multiple_of(mine * sub // LANES * LANES, LANES)
     within = lax.rem(mine * sub, LANES)
     slot = lax.broadcasted_iota(jnp.int32, (LANES, LANES), 0)
     each = 8
     picked = chunks if per > 1 else chunks - 1
 
-    def prepare():
+    @pl.when(works)
+    def _():
         for copy in hop_copies:
             copy.wait()
         for k in range(fan2 + 1):
@@ -303,6 +229,96 @@
                         row = jnp.where(inside, turned[q][j : j + 1], row)
                 hop_rows[c, k : k + 1, :] = row
 
+    pl.semaphore_wait(barrier, nd + nf - 2)
+
+    for d, t in peers:
+        pl.semaphore_signal(ready, inc=1, device_id={"dom": dom_at(d, t)}, device_id_type=MESH)
+    wants = {}
+    for d, t in peers:
+        where = {"dom": dom_at(d, t)}
+        to = dom_at(d, t)
+        sem = want_sm_send.at[d, t], want_sm_recv.at[d, t]
+        wants[d, t] = [
+            remote(ask_row.at[to], got_sm.at[d, t], *sem, where),
+            remote(ask.at[to], got.at[d, t], want_send.at[d, t], want_recv.at[d, t], where),
+        ]
+    own_sm = local(13, ask_row.at[me], got_sm.at[0, 0])
+    got[0, 0] = ask[me]
+    for copy in early_copies:
+        copy.wait()
+    buddy = {"dom": dom_at(0, 1)}
+
+    def to_worker(w, src, dst, send, recv, where):
+        copy = pltpu.make_async_remote_copy(
+            src_ref=src,
+            dst_ref=dst,
+            send_sem=send,
+            recv_sem=recv,
+            device_id={**where, "feat": first + w},
+            device_id_type=MESH,
+        )
+        pl.when(mf != first + w)(copy.start)
+        loose.append((w, copy))
+
+    def landed(ref, sem, f):
+        copy = pltpu.make_async_copy(ref, ref, sem)
+        pl.when(mf != f)(copy.wait)
+
+    loose = []
+    for w in range(workers):
+        for i, ref in enumerate((b1_all.at[mf], b2_all.at[mf], w2_all.at[odd, mf])):
+            to_worker(w, ref, ref, early_send.at[w, i], early_recv.at[mf, i], {})
+
+    def gather(jobs):
+        for slot, read, _ in jobs:
+            for k in range(LANES):
+                rows_vm[slot, k : k + 1, :] = table[pl.ds(read(k), 1), :]
+        blocks = []
+        for slot, _, wanted in jobs:
+            turned = jnp.transpose(rows_vm[slot])
+            piece = wanted >> (table_rows.bit_length() - 1)
+            block = jnp.zeros((height, LANES), F32)
+            for p in range(pieces):
+                block = jnp.where(piece == p, turned[p * height : (p + 1) * height], block)
+            blocks.append(block.astype(BF16))
+        return blocks
+
+    for copy in seed_local:
+        copy.wait()
+    def seed_job(g):
+        at = g * LANES
+        return (
+            nd + g,
+            lambda k: seed_sm[0, at + k] & (table_rows - 1),
+            seed_vm[:, at : at + LANES],
+        )
+
+    for g, block in enumerate(gather([seed_job(g) for g in range(groups)])):
+        seed_own[g] = block
+    for w in range(workers):
+        block = seed_own.at[w * sub // LANES]
+        to_worker(w, block, seed_all.at[mf], seed_send.at[w], seed_recv.at[mf], {})
+
+    @pl.when(works)
+    def _():
+        seed_all[mf] = seed_own[mine * sub // LANES]
+
+    steps = min(4, pairs)
+    ends = [nd * i // steps for i in range(steps + 1)]
+
+    def expand(i, c):
+        columns = slice(c * LANES, (c + 1) * LANES)
+        short = jnp.int16
+        row = jnp.broadcast_to(hop_rows[c, fan2 : fan2 + 1, :], (16, LANES)).astype(short)
+        row = jnp.concatenate([row] * (LANES // 16), axis=0)
+        for o in range(ends[i], ends[i + 1]):
+            these = slice(o * LANES, (o + 1) * LANES)
+            count = lax.shift_right_logical(words[o // each, :, columns], o % each * 4) & 15
+            pick_two[these, columns] = count.astype(F32).astype(BF16)
+            same = row == (slot + o * LANES).astype(short)
+            pick_one[these, columns] = jnp.where(same, jnp.ones((), BF16), jnp.zeros((), BF16))
+
+    def prepare():
         for c in range(picked):
             columns = slice(c * LANES, (c + 1) * LANES)
             for g in range(words.shape[0]):
@@ -315,26 +331,7 @@
                     count = count + jnp.where((row & (LANES - 1)) == slot, unit, 0)
                 words[g, :, columns] = count
 
-    @pl.when(works)
-    def _():
-        prepare()
-
     def work():
-        def expand(owners):
-            for o in owners:
-                place = slot + o * LANES
-                these = slice(o * LANES, (o + 1) * LANES)
-                for c in range(picked):
-                    columns = slice(c * LANES, (c + 1) * LANES)
-                    count = lax.shift_right_logical(words[o // each, :, columns], o % each * 4)
-                    pick_two[these, columns] = (count & 15).astype(F32).astype(BF16)
-                    pick_one[these, columns] = jnp.where(
-                        hop_rows[c, fan2 : fan2 + 1, :] == place, 1.0, 0.0
-                    ).astype(BF16)
-
-        steps = min(4, pairs)
-        ends = [nd * i // steps for i in range(steps + 1)]
-        expand(range(ends[0], ends[1]))
         for f in range(nf):
             for i, ref in enumerate((b1_all.at[f], b2_all.at[f], w2_all.at[odd, f])):
                 landed(ref, early_recv.at[f, i], f)
@@ -342,12 +339,6 @@
         for d in range(1, nf):
             ref = w2_all.at[odd, feat_at(d)]
             swaps.append(remote(ref, ref, pair_send.at[d], pair_recv.at[d], buddy))
-        for copy in weight_copies:
-            copy.wait()
-        for copy in swaps:
-            copy.wait_recv()
-        w2_full[...] = jnp.transpose(w2_all[...].reshape(2 * hid, w2_all.shape[3]))
-
         def column(rows):
             return jnp.concatenate(
                 [jnp.transpose(jnp.broadcast_to(rows[f], (LANES, hid_dev))) for f in range(nf)], axis=0
@@ -355,6 +346,8 @@
 
         b1 = column(b1_all)
         b2 = column(b2_all)
+        for c in range(picked if steps > 1 else 0):
+            expand(1, c)
         for f in range(nf):
             landed(seed_all.at[f], seed_recv.at[f], f)
 
@@ -372,8 +365,15 @@
         done = 0
         for i in range(steps):
             part = [(o // 2, o % 2) for o in range(ends[i], ends[i + 1])]
-            if i + 1 < steps:
-                expand(range(ends[i + 1], ends[i + 2]))
+            if i == 1:
+                for later in range(2, steps):
+                    for c in range(picked):
+                        expand(later, c)
+                for copy in weight_copies:
+                    copy.wait()
+                for copy in swaps:
+                    copy.wait_recv()
+                w2_full[...] = jnp.transpose(w2_all[...].reshape(2 * hid, w2_all.shape[3]))
             for d, t in part:
                 for f in range(nf):
                     if d or t:
@@ -458,7 +458,7 @@
     def want_job(d, t):
         return (2 * d + t, lambda k: got_sm[d, t, 0, k], got[d, t])
 
-    for d in range(pairs):
+    def serve(d):
         for t in range(2):
             if d or t:
                 for copy in wants[d, t]:
@@ -467,17 +467,39 @@
                 own_sm.wait()
         for t, block in enumerate(gather([want_job(d, t) for t in range(2)])):
             served[d, t] = block
-            for w in range(workers):
-                block = served.at[d, t]
-                spot = everyone.at[d, t, mf]
-                send = data_send.at[d, t, w]
-                recv = data_recv.at[d, t, mf]
-                if d or t:
-                    where = {"dom": dom_at(d, t), "feat": first + w}
-                    data.append(remote(block, spot, send, recv, where))
-                else:
-                    to_worker(w, block, spot, send, recv, {})
+            if d:
+                deliver(d, t)
+
+    def deliver(d, t):
+        for w in range(workers):
+            block = served.at[d, t]
+            spot = everyone.at[d, t, mf]
+            send = data_send.at[d, t, w]
+            recv = data_recv.at[d, t, mf]
+            if d or t:
+                where = {"dom": dom_at(d, t), "feat": first + w}
+                data.append(remote(block, spot, send, recv, where))
+            else:
+                to_worker(w, block, spot, send, recv, {})
+
+    serve(0)
+    deliver(0, 0)
     everyone[0, 0, mf] = served[0, 0]
+
+    @pl.when(works)
+    def _():
+        prepare()
+
+    pl.semaphore_wait(ready, nd - 1)
+    deliver(0, 1)
+
+    @pl.when(works)
+    def _():
+        for c in range(picked):
+            expand(0, c)
+
+    for d in range(1, pairs):
+        serve(d)
 
     @pl.when(works)
     def _():

time: 21.9 us -> 20.7 us (0.945)
  Pallas kernels: 21.1 us -> 19.9 us
    pallas_call x1, Pallas kernels: 21.1 us -> 19.9 us  [per_device(): pl.pallas_call(functools.partial(kernel, nd, nf), out_shape=pltpu.VMEM((h...]
where the time goes in v4:
time: 20.7 us; the launch traced here: 20.5 us
  Pallas kernels  19.9 us (96%)
  local copies, waits for them, and re-layouts  0.63 us (3%)
    pallas_call x1, Pallas kernels, per_device(): pl.pallas_call(functools.partial(kernel, nd, nf), out_shape=pltpu.VMEM((h...  19.9 us
    unnamed x1, local copies, waits for them, and re-layouts  0.63 us

profile of v4, /device:TPU:0, one launch (start us, length us, event | category | flops | bytes accessed | tf_op | source)
XLA Modules:
  0.0 20.5 jit_solution(7818560129611394709)
XLA Ops:
  0.0 19.9 %shard_map.118 = f32[64,256]{1,0:T(8,128)S(1)} custom-call(bf16[32,16384]{1,0:T(8,128)(2,1)} %feat_hbm.1, s32[1,256]{1,0:T(1,128)} %bitcast.7, s32[1,8,128]{2,1,0:T(8,128)} %want_hbm.1, s32[1,8]{1,0:T(1,128)} %live_hbm.1, s32[15,256]{1,0:T(8,128)} %one_hbm.1, s32[10,15,256]{2,1,0:T(8,128)} %two_hbm.1, bf16[256,128]{1,0:T(8,128)(2,1)} %w1s_hbm.1, ...), custom_call_target="tpu_custom_call" | custom-call | tf_op jit(solution)/shard_map/pallas_call | solution.py:554
  19.9 0.6 %copy.14 = f32[64,256]{1,0:T(8,128)} copy(f32[64,256]{1,0:T(8,128)S(1)} %shard_map.118) | data formatting | bytes 131072

commit v5 on v4

--- a/solution.py
+++ b/solution.py
@@ -45,8 +45,7 @@
     one_ref,
     two_ref,
     w1_ref,
-    ask,
-    ask_row,
+    asks,
     got,
     got_sm,
     table,
@@ -56,8 +55,7 @@
     seed_own,
     seed_all,
     w2_all,
-    b1_all,
-    b2_all,
+    b_all,
     hop_rows,
     words,
     pick_one,
@@ -72,18 +70,10 @@
     ready,
     want_send,
     want_recv,
-    want_sm_send,
-    want_sm_recv,
     data_send,
     data_recv,
-    seed_send,
-    seed_recv,
-    early_send,
-    early_recv,
-    pair_send,
-    pair_recv,
-    z_send,
-    z_recv,
+    side_send,
+    side_recv,
 ):
     height, nodes = feat_vm.shape
     fan1, seeds = one_ref.shape
@@ -138,21 +128,21 @@
 
     want_copies = [local(0, want_hbm.at[0], want_vm), local(1, live_hbm, live_sm)]
     feat_copy = local(2, feat_hbm, feat_vm)
-    early_copies = [
-        local(3, w2s_hbm, w2_all.at[0, mf]),
-        local(4, w2n_hbm, w2_all.at[1, mf]),
-        local(5, b1_hbm, b1_all.at[mf]),
-        local(6, b2_hbm, b2_all.at[mf]),
-    ]
-    seed_local = [local(7, seed_hbm, seed_vm), local(8, seed_hbm, seed_sm)]
+    for i, (b_hbm, w2_hbm) in enumerate(((b1_hbm, w2s_hbm), (b2_hbm, w2n_hbm))):
+        local(3, b_hbm, b_all.at[i, mf])
+        local(4, w2_hbm, w2_all.at[i, mf])
+    seed_local = [local(5, seed_hbm, seed_vm), local(6, seed_hbm, seed_sm)]
     hop_copies = [
-        pltpu.make_async_copy(one_hbm, one_ref, local_sem.at[9]),
-        pltpu.make_async_copy(two_hbm, two_ref, local_sem.at[10]),
+        pltpu.make_async_copy(one_hbm, one_ref, local_sem.at[7]),
+        pltpu.make_async_copy(two_hbm, two_ref, local_sem.at[8]),
     ]
     weight_copies = [
-        pltpu.make_async_copy(w1s_hbm, w1_ref.at[:, :depth], local_sem.at[11]),
-        pltpu.make_async_copy(w1n_hbm, w1_ref.at[:, depth:], local_sem.at[12]),
+        pltpu.make_async_copy(w1s_hbm, w1_ref.at[:, :depth], local_sem.at[9]),
+        pltpu.make_async_copy(w1n_hbm, w1_ref.at[:, depth:], local_sem.at[9]),
     ]
+
+    def drain(ref, sem):
+        pltpu.make_async_copy(ref, ref, sem).wait()
 
     @pl.when(works)
     def _():
@@ -176,8 +166,8 @@
         copy.wait()
     for o in range(nd):
         wanted = jnp.where(lane < live_sm[0, o], want_vm[o : o + 1], -1)
-        ask[o] = wanted
-        ask_row[o] = wanted & (table_rows - 1)
+        asks[0, o] = wanted
+        asks[1, o] = wanted & (table_rows - 1)
     feat_copy.wait()
     tiles = table_rows // LANES
     step = min(8, tiles)
@@ -233,19 +223,15 @@
 
     for d, t in peers:
         pl.semaphore_signal(ready, inc=1, device_id={"dom": dom_at(d, t)}, device_id_type=MESH)
-    wants = {}
     for d, t in peers:
         where = {"dom": dom_at(d, t)}
         to = dom_at(d, t)
-        sem = want_sm_send.at[d, t], want_sm_recv.at[d, t]
-        wants[d, t] = [
-            remote(ask_row.at[to], got_sm.at[d, t], *sem, where),
-            remote(ask.at[to], got.at[d, t], want_send.at[d, t], want_recv.at[d, t], where),
-        ]
-    own_sm = local(13, ask_row.at[me], got_sm.at[0, 0])
-    got[0, 0] = ask[me]
-    for copy in early_copies:
-        copy.wait()
+        remote(asks.at[0, to], got.at[d, t], want_send.at[0], want_recv.at[0, d], where)
+        remote(asks.at[1, to], got_sm.at[d, t], want_send.at[1], want_recv.at[1, d], where)
+    own_sm = local(10, asks.at[1, me], got_sm.at[0, 0])
+    got[0, 0] = asks[0, me]
+    drain(b_all.at[:, mf], local_sem.at[3])
+    drain(w2_all.at[:, mf], local_sem.at[4])
     buddy = {"dom": dom_at(0, 1)}
 
     def to_worker(w, src, dst, send, recv, where):
@@ -258,16 +244,10 @@
             device_id_type=MESH,
         )
         pl.when(mf != first + w)(copy.start)
-        loose.append((w, copy))
-
-    def landed(ref, sem, f):
-        copy = pltpu.make_async_copy(ref, ref, sem)
-        pl.when(mf != f)(copy.wait)
-
-    loose = []
+
     for w in range(workers):
-        for i, ref in enumerate((b1_all.at[mf], b2_all.at[mf], w2_all.at[odd, mf])):
-            to_worker(w, ref, ref, early_send.at[w, i], early_recv.at[mf, i], {})
+        for ref, i in ((b_all.at[0, mf], 0), (b_all.at[1, mf], 0), (w2_all.at[odd, mf], 1)):
+            to_worker(w, ref, ref, side_send.at[i], side_recv.at[i], {})
 
     def gather(jobs):
         for slot, read, _ in jobs:
@@ -297,7 +277,7 @@
         seed_own[g] = block
     for w in range(workers):
         block = seed_own.at[w * sub // LANES]
-        to_worker(w, block, seed_all.at[mf], seed_send.at[w], seed_recv.at[mf], {})
+        to_worker(w, block, seed_all.at[mf], side_send.at[2], side_recv.at[2], {})
 
     @pl.when(works)
     def _():
@@ -330,26 +310,26 @@
                     unit = jnp.where(real, jnp.left_shift(1, (rel & (each - 1)) * 4), 0)
                     count = count + jnp.where((row & (LANES - 1)) == slot, unit, 0)
                 words[g, :, columns] = count
+        for c in range(picked):
+            expand(0, c)
 
     def work():
-        for f in range(nf):
-            for i, ref in enumerate((b1_all.at[f], b2_all.at[f], w2_all.at[odd, f])):
-                landed(ref, early_recv.at[f, i], f)
-        swaps = []
+        drain(b_all.at[:, : nf - 1], side_recv.at[0])
+        drain(w2_all.at[0, : nf - 1], side_recv.at[1])
         for d in range(1, nf):
             ref = w2_all.at[odd, feat_at(d)]
-            swaps.append(remote(ref, ref, pair_send.at[d], pair_recv.at[d], buddy))
+            remote(ref, ref, side_send.at[4], side_recv.at[3], buddy)
+
         def column(rows):
             return jnp.concatenate(
                 [jnp.transpose(jnp.broadcast_to(rows[f], (LANES, hid_dev))) for f in range(nf)], axis=0
             )
 
-        b1 = column(b1_all)
-        b2 = column(b2_all)
+        b1 = column(b_all[0])
+        b2 = column(b_all[1])
         for c in range(picked if steps > 1 else 0):
             expand(1, c)
-        for f in range(nf):
-            landed(seed_all.at[f], seed_recv.at[f], f)
+        drain(seed_all.at[: nf - 1], side_recv.at[2])
 
         def whole(blocks):
             if height % 16:
@@ -369,18 +349,15 @@
                 for later in range(2, steps):
                     for c in range(picked):
                         expand(later, c)
-                for copy in weight_copies:
-                    copy.wait()
-                for copy in swaps:
-                    copy.wait_recv()
+                drain(w1_ref, local_sem.at[9])
+                drain(w2_all.at[0, : nf - 1], side_recv.at[3])
                 w2_full[...] = jnp.transpose(w2_all[...].reshape(2 * hid, w2_all.shape[3]))
-            for d, t in part:
-                for f in range(nf):
-                    if d or t:
-                        spot = everyone.at[d, t, f]
-                        pltpu.make_async_copy(spot, spot, data_recv.at[d, t, f]).wait()
-                    else:
-                        landed(everyone.at[0, 0, f], data_recv.at[0, 0, f], f)
+            for d in range(ends[i] // 2, ends[i + 1] // 2):
+                if d:
+                    drain(everyone.at[d], data_recv.at[d])
+                else:
+                    drain(everyone.at[0, 0, : nf - 1], data_recv.at[0])
+                    drain(everyone.at[0, 1], data_recv.at[pairs])
             fetched = jnp.concatenate([whole(everyone[d, t]) for d, t in part], axis=1)
             these = slice(done, done + len(part) * LANES)
             done += len(part) * LANES
@@ -445,44 +422,38 @@
                 packed = jnp.where((lane >= p * sub) & (lane < (p + 1) * sub), value, packed)
             z_own[f] = packed
 
-        z_copies = []
         for e in range(1, nf):
             to = feat_at(e)
             where = {"feat": to}
-            z_copies.append(remote(z_own.at[to], z_all.at[mine], z_send.at[e], z_recv.at[mine], where))
+            remote(z_own.at[to], z_all.at[mine], side_send.at[5], side_recv.at[4], where)
         z_all[mine] = z_own[mf]
-        for copy in swaps + z_copies:
-            copy.wait_send()
-
-    data = []
+
     def want_job(d, t):
         return (2 * d + t, lambda k: got_sm[d, t, 0, k], got[d, t])
 
-    def serve(d):
-        for t in range(2):
-            if d or t:
-                for copy in wants[d, t]:
-                    copy.wait_recv()
-            else:
-                own_sm.wait()
-        for t, block in enumerate(gather([want_job(d, t) for t in range(2)])):
-            served[d, t] = block
-            if d:
-                deliver(d, t)
+    def arrived(d, these):
+        for i, ref in enumerate((got, got_sm)):
+            pltpu.make_async_remote_copy(
+                src_ref=asks.at[i, these],
+                dst_ref=ref.at[d, these],
+                send_sem=want_send.at[i],
+                recv_sem=want_recv.at[i, d],
+                device_id=buddy,
+                device_id_type=MESH,
+            ).wait_recv()
 
     def deliver(d, t):
         for w in range(workers):
             block = served.at[d, t]
             spot = everyone.at[d, t, mf]
-            send = data_send.at[d, t, w]
-            recv = data_recv.at[d, t, mf]
             if d or t:
                 where = {"dom": dom_at(d, t), "feat": first + w}
-                data.append(remote(block, spot, send, recv, where))
+                remote(block, spot, data_send.at[min(d, 1)], data_recv.at[d or pairs], where)
             else:
-                to_worker(w, block, spot, send, recv, {})
-
-    serve(0)
+                to_worker(w, block, spot, side_send.at[3], data_recv.at[0], {})
+
+    own_sm.wait()
+    served[0, 0] = gather([want_job(0, 0)])[0]
     deliver(0, 0)
     everyone[0, 0, mf] = served[0, 0]
 
@@ -490,27 +461,43 @@
     def _():
         prepare()
 
+    arrived(0, slice(1, 2))
+    served[0, 1] = gather([want_job(0, 1)])[0]
     pl.semaphore_wait(ready, nd - 1)
     deliver(0, 1)
-
-    @pl.when(works)
-    def _():
-        for c in range(picked):
-            expand(0, c)
-
     for d in range(1, pairs):
-        serve(d)
+        arrived(d, slice(0, 2))
+        for t, block in enumerate(gather([want_job(d, t) for t in range(2)])):
+            served[d, t] = block
+            deliver(d, t)
 
     @pl.when(works)
     def _():
         work()
 
-    for w, copy in loose:
-        pl.when(mf != first + w)(copy.wait_send)
-    for copy in data + [copy for both in wants.values() for copy in both]:
-        copy.wait_send()
-    for w in range(workers):
-        landed(z_all.at[w], z_recv.at[w], first + w)
+    def sent(n):
+        drain(b_all.at[:, :n], side_send.at[0])
+        drain(w2_all.at[0, :n], side_send.at[1])
+        drain(seed_all.at[:n], side_send.at[2])
+        drain(everyone.at[0, 0, :n], side_send.at[3])
+
+    drain(asks.at[0, : nd - 1], want_send.at[0])
+    drain(asks.at[1, : nd - 1], want_send.at[1])
+    drain(everyone.at[0, 1, :workers], data_send.at[0])
+    drain(everyone.at[1:, :, :workers], data_send.at[1])
+
+    @pl.when(works)
+    def _():
+        sent(workers - 1)
+        drain(w2_all.at[0, : nf - 1], side_send.at[4])
+        drain(z_own.at[: nf - 1], side_send.at[5])
+        drain(z_all.at[: workers - 1], side_recv.at[4])
+
+    @pl.when(jnp.logical_not(works))
+    def _():
+        sent(workers)
+        drain(z_all, side_recv.at[4])
+
     for g in range(groups):
         for p in range(per):
             block = jnp.zeros((part_rows, LANES), F32)
@@ -565,8 +552,7 @@
             pltpu.VMEM(hop_one.shape, jnp.int32),
             pltpu.VMEM(hop_two.shape, jnp.int32),
             pltpu.VMEM((hid, 2 * depth), BF16),
-            pltpu.VMEM((nd, 1, cap), jnp.int32),
-            pltpu.VMEM((nd, 1, cap), jnp.int32),
+            pltpu.VMEM((2, nd, 1, cap), jnp.int32),
             pltpu.VMEM((nd // 2, 2, 1, cap), jnp.int32),
             pltpu.SMEM((nd // 2, 2, 1, cap), jnp.int32),
             pltpu.VMEM((nodes * height // depth, LANES), F32),
@@ -576,8 +562,7 @@
             pltpu.VMEM((groups, height, LANES), BF16),
             pltpu.VMEM((nf, height, LANES), BF16),
             pltpu.VMEM((2, nf, hid_dev, w2_self.shape[0]), BF16),
-            pltpu.VMEM((nf, 1, hid_dev), F32),
-            pltpu.VMEM((nf, 1, hid_dev), F32),
+            pltpu.VMEM((2, nf, 1, hid_dev), F32),
             pltpu.VMEM((columns // LANES, 16, LANES), jnp.int32),
             pltpu.VMEM((pl.cdiv(nd, 8), LANES, columns), jnp.int32),
             pltpu.VMEM((nd * cap, columns), BF16),
@@ -588,15 +573,15 @@
             pltpu.VMEM((hid, 2 * hid), BF16),
             pltpu.VMEM((nf,) + result, F32),
             pltpu.VMEM((workers,) + result, F32),
-            dma((14,)),
+            dma((11,)),
             pltpu.SemaphoreType.REGULAR,
-        ]
-        + [dma((nd // 2, 2))] * 4
-        + [dma((nd // 2, 2, workers)), dma((nd // 2, 2, nf))]
-        + [dma((workers,)), dma((nf,))]
-        + [dma((workers, 3)), dma((nf, 3))]
-        + [dma((nf,))] * 2
-        + [dma((nf,)), dma((workers,))],
+            dma((2,)),
+            dma((2, nd // 2)),
+            dma((2,)),
+            dma((nd // 2 + 1,)),
+            dma((6,)),
+            dma((5,)),
+        ],
         compiler_params=pltpu.CompilerParams(collective_id=0, has_side_effects=True),
     )(
         features,

time: 20.7 us -> 19.7 us (0.952)
  Pallas kernels: 19.9 us -> 18.9 us
    pallas_call x1, Pallas kernels: 19.9 us -> 18.9 us  [per_device(): pl.pallas_call(functools.partial(kernel, nd, nf), out_shape=pltpu.VMEM((h...]
where the time goes in v5:
time: 19.7 us; the launch traced here: 19.5 us
  Pallas kernels  18.9 us (96%)
  local copies, waits for them, and re-layouts  0.63 us (3%)
    pallas_call x1, Pallas kernels, per_device(): pl.pallas_call(functools.partial(kernel, nd, nf), out_shape=pltpu.VMEM((h...  18.9 us
    unnamed x1, local copies, waits for them, and re-layouts  0.63 us

profile of v5, /device:TPU:0, one launch (start us, length us, event | category | flops | bytes accessed | tf_op | source)
XLA Modules:
  0.0 19.5 jit_solution(16767954741388367012)
XLA Ops:
  0.0 18.9 %shard_map.118 = f32[64,256]{1,0:T(8,128)S(1)} custom-call(bf16[32,16384]{1,0:T(8,128)(2,1)} %feat_hbm.1, s32[1,256]{1,0:T(1,128)} %bitcast.7, s32[1,8,128]{2,1,0:T(8,128)} %want_hbm.1, s32[1,8]{1,0:T(1,128)} %live_hbm.1, s32[15,256]{1,0:T(8,128)} %one_hbm.1, s32[10,15,256]{2,1,0:T(8,128)} %two_hbm.1, bf16[256,128]{1,0:T(8,128)(2,1)} %w1s_hbm.1, ...), custom_call_target="tpu_custom_call" | custom-call | tf_op jit(solution)/shard_map/pallas_call | solution.py:541
  18.9 0.6 %copy.14 = f32[64,256]{1,0:T(8,128)} copy(f32[64,256]{1,0:T(8,128)S(1)} %shard_map.118) | data formatting | bytes 131072

commit v6 on v5

--- a/solution.py
+++ b/solution.py
@@ -189,14 +189,91 @@
 
     lax.fori_loop(0, tiles // step, turn, 0)
 
+    pl.semaphore_wait(barrier, nd + nf - 2)
+
+    for d, t in peers:
+        pl.semaphore_signal(ready, inc=1, device_id={"dom": dom_at(d, t)}, device_id_type=MESH)
+    for d, t in peers:
+        where = {"dom": dom_at(d, t)}
+        to = dom_at(d, t)
+        remote(asks.at[0, to], got.at[d, t], want_send.at[0], want_recv.at[0, d], where)
+        remote(asks.at[1, to], got_sm.at[d, t], want_send.at[1], want_recv.at[1, d], where)
+    own_sm = local(10, asks.at[1, me], got_sm.at[0, 0])
+    got[0, 0] = asks[0, me]
+    drain(b_all.at[:, mf], local_sem.at[3])
+    drain(w2_all.at[:, mf], local_sem.at[4])
+    buddy = {"dom": dom_at(0, 1)}
+
+    def to_worker(w, src, dst, send, recv, where):
+        copy = pltpu.make_async_remote_copy(
+            src_ref=src,
+            dst_ref=dst,
+            send_sem=send,
+            recv_sem=recv,
+            device_id={**where, "feat": first + w},
+            device_id_type=MESH,
+        )
+        pl.when(mf != first + w)(copy.start)
+
+    for w in range(workers):
+        for ref, i in ((b_all.at[0, mf], 0), (b_all.at[1, mf], 0), (w2_all.at[odd, mf], 1)):
+            to_worker(w, ref, ref, side_send.at[i], side_recv.at[i], {})
+
+    def gather(jobs):
+        for slot, read, _ in jobs:
+            for k in range(LANES):
+                rows_vm[slot, k : k + 1, :] = table[pl.ds(read(k), 1), :]
+        blocks = []
+        for slot, _, wanted in jobs:
+            turned = jnp.transpose(rows_vm[slot])
+            piece = wanted >> (table_rows.bit_length() - 1)
+            block = jnp.zeros((height, LANES), F32)
+            for p in range(pieces):
+                block = jnp.where(piece == p, turned[p * height : (p + 1) * height], block)
+            blocks.append(block.astype(BF16))
+        return blocks
+
+    for copy in seed_local:
+        copy.wait()
+    def seed_job(g):
+        at = g * LANES
+        return (
+            nd + g,
+            lambda k: seed_sm[0, at + k] & (table_rows - 1),
+            seed_vm[:, at : at + LANES],
+        )
+
+    for g, block in enumerate(gather([seed_job(g) for g in range(groups)])):
+        seed_own[g] = block
+    for w in range(workers):
+        block = seed_own.at[w * sub // LANES]
+        to_worker(w, block, seed_all.at[mf], side_send.at[2], side_recv.at[2], {})
+
+    @pl.when(works)
+    def _():
+        seed_all[mf] = seed_own[mine * sub // LANES]
+
     base = pl.multiple_of(mine * sub // LANES * LANES, LANES)
     within = lax.rem(mine * sub, LANES)
     slot = lax.broadcasted_iota(jnp.int32, (LANES, LANES), 0)
     each = 8
     picked = chunks if per > 1 else chunks - 1
-
-    @pl.when(works)
-    def _():
+    steps = min(4, pairs)
+    ends = [nd * i // steps for i in range(steps + 1)]
+
+    def expand(owners, c):
+        columns = slice(c * LANES, (c + 1) * LANES)
+        short = jnp.int16
+        row = jnp.broadcast_to(hop_rows[c, fan2 : fan2 + 1, :], (16, LANES)).astype(short)
+        row = jnp.concatenate([row] * (LANES // 16), axis=0)
+        for o in owners:
+            these = slice(o * LANES, (o + 1) * LANES)
+            count = lax.shift_right_logical(words[o // each, :, columns], o % each * 4) & 15
+            pick_two[these, columns] = count.astype(F32).astype(BF16)
+            same = row == (slot + o * LANES).astype(short)
+            pick_one[these, columns] = jnp.where(same, jnp.ones((), BF16), jnp.zeros((), BF16))
+
+    def prepare():
         for copy in hop_copies:
             copy.wait()
         for k in range(fan2 + 1):
@@ -218,87 +295,6 @@
                         inside = (lane >= q * sub) & (lane < (q + 1) * sub)
                         row = jnp.where(inside, turned[q][j : j + 1], row)
                 hop_rows[c, k : k + 1, :] = row
-
-    pl.semaphore_wait(barrier, nd + nf - 2)
-
-    for d, t in peers:
-        pl.semaphore_signal(ready, inc=1, device_id={"dom": dom_at(d, t)}, device_id_type=MESH)
-    for d, t in peers:
-        where = {"dom": dom_at(d, t)}
-        to = dom_at(d, t)
-        remote(asks.at[0, to], got.at[d, t], want_send.at[0], want_recv.at[0, d], where)
-        remote(asks.at[1, to], got_sm.at[d, t], want_send.at[1], want_recv.at[1, d], where)
-    own_sm = local(10, asks.at[1, me], got_sm.at[0, 0])
-    got[0, 0] = asks[0, me]
-    drain(b_all.at[:, mf], local_sem.at[3])
-    drain(w2_all.at[:, mf], local_sem.at[4])
-    buddy = {"dom": dom_at(0, 1)}
-
-    def to_worker(w, src, dst, send, recv, where):
-        copy = pltpu.make_async_remote_copy(
-            src_ref=src,
-            dst_ref=dst,
-            send_sem=send,
-            recv_sem=recv,
-            device_id={**where, "feat": first + w},
-            device_id_type=MESH,
-        )
-        pl.when(mf != first + w)(copy.start)
-
-    for w in range(workers):
-        for ref, i in ((b_all.at[0, mf], 0), (b_all.at[1, mf], 0), (w2_all.at[odd, mf], 1)):
-            to_worker(w, ref, ref, side_send.at[i], side_recv.at[i], {})
-
-    def gather(jobs):
-        for slot, read, _ in jobs:
-            for k in range(LANES):
-                rows_vm[slot, k : k + 1, :] = table[pl.ds(read(k), 1), :]
-        blocks = []
-        for slot, _, wanted in jobs:
-            turned = jnp.transpose(rows_vm[slot])
-            piece = wanted >> (table_rows.bit_length() - 1)
-            block = jnp.zeros((height, LANES), F32)
-            for p in range(pieces):
-                block = jnp.where(piece == p, turned[p * height : (p + 1) * height], block)
-            blocks.append(block.astype(BF16))
-        return blocks
-
-    for copy in seed_local:
-        copy.wait()
-    def seed_job(g):
-        at = g * LANES
-        return (
-            nd + g,
-            lambda k: seed_sm[0, at + k] & (table_rows - 1),
-            seed_vm[:, at : at + LANES],
-        )
-
-    for g, block in enumerate(gather([seed_job(g) for g in range(groups)])):
-        seed_own[g] = block
-    for w in range(workers):
-        block = seed_own.at[w * sub // LANES]
-        to_worker(w, block, seed_all.at[mf], side_send.at[2], side_recv.at[2], {})
-
-    @pl.when(works)
-    def _():
-        seed_all[mf] = seed_own[mine * sub // LANES]
-
-    steps = min(4, pairs)
-    ends = [nd * i // steps for i in range(steps + 1)]
-
-    def expand(i, c):
-        columns = slice(c * LANES, (c + 1) * LANES)
-        short = jnp.int16
-        row = jnp.broadcast_to(hop_rows[c, fan2 : fan2 + 1, :], (16, LANES)).astype(short)
-        row = jnp.concatenate([row] * (LANES // 16), axis=0)
-        for o in range(ends[i], ends[i + 1]):
-            these = slice(o * LANES, (o + 1) * LANES)
-            count = lax.shift_right_logical(words[o // each, :, columns], o % each * 4) & 15
-            pick_two[these, columns] = count.astype(F32).astype(BF16)
-            same = row == (slot + o * LANES).astype(short)
-            pick_one[these, columns] = jnp.where(same, jnp.ones((), BF16), jnp.zeros((), BF16))
-
-    def prepare():
         for c in range(picked):
             columns = slice(c * LANES, (c + 1) * LANES)
             for g in range(words.shape[0]):
@@ -310,10 +306,10 @@
                     unit = jnp.where(real, jnp.left_shift(1, (rel & (each - 1)) * 4), 0)
                     count = count + jnp.where((row & (LANES - 1)) == slot, unit, 0)
                 words[g, :, columns] = count
+
+    def work():
         for c in range(picked):
-            expand(0, c)
-
-    def work():
+            expand(range(ends[1]), c)
         drain(b_all.at[:, : nf - 1], side_recv.at[0])
         drain(w2_all.at[0, : nf - 1], side_recv.at[1])
         for d in range(1, nf):
@@ -327,8 +323,13 @@
 
         b1 = column(b_all[0])
         b2 = column(b_all[1])
-        for c in range(picked if steps > 1 else 0):
-            expand(1, c)
+        for c in range(picked):
+            expand(range(ends[1], ends[2]), c)
+        for c in range(picked):
+            expand(range(ends[2], nd), c)
+        drain(w1_ref, local_sem.at[9])
+        drain(w2_all.at[0, : nf - 1], side_recv.at[3])
+        w2_full[...] = jnp.transpose(w2_all[...].reshape(2 * hid, w2_all.shape[3]))
         drain(seed_all.at[: nf - 1], side_recv.at[2])
 
         def whole(blocks):
@@ -340,18 +341,23 @@
         if per > 1:
             x_seed = pltpu.roll(x_seed, lax.rem(2 * LANES - sub - within, LANES), 1)
 
-        wide = 2 * LANES
+        def fold(value):
+            width = sub
+            while width < LANES:
+                value = value + pltpu.roll(value, width, 1)
+                width *= 2
+            return value
+
+        def layer(n):
+            columns = slice(n * LANES, (n + 2) * LANES)
+            pre = jnp.dot(w1_ref[...], xm_all[:, columns], preferred_element_type=F32)
+            return jnp.maximum(pre[:, :LANES] + b1, 0.0), jnp.maximum(pre[:, LANES:] + b1, 0.0)
+
         total = jnp.zeros((depth, LANES), F32)
+        summed = jnp.zeros((hid, LANES), F32)
         done = 0
         for i in range(steps):
             part = [(o // 2, o % 2) for o in range(ends[i], ends[i + 1])]
-            if i == 1:
-                for later in range(2, steps):
-                    for c in range(picked):
-                        expand(later, c)
-                drain(w1_ref, local_sem.at[9])
-                drain(w2_all.at[0, : nf - 1], side_recv.at[3])
-                w2_full[...] = jnp.transpose(w2_all[...].reshape(2 * hid, w2_all.shape[3]))
             for d in range(ends[i] // 2, ends[i + 1] // 2):
                 if d:
                     drain(everyone.at[d], data_recv.at[d])
@@ -377,13 +383,6 @@
                 xm_all[:depth, columns] = own.astype(BF16)
                 xm_all[depth:, columns] = (mean * (1.0 / fan2)).astype(BF16)
 
-        def fold(value):
-            width = sub
-            while width < LANES:
-                value = value + pltpu.roll(value, width, 1)
-                width *= 2
-            return value
-
         is_seed = lane >= LANES - sub
         last = slice((chunks - 1) * LANES, chunks * LANES)
         m_one = fold(total) * (1.0 / fan1)
@@ -393,17 +392,12 @@
         xm_all[:depth, last] = x_seed.astype(BF16)
         xm_all[depth:, last] = m_one.astype(BF16)
 
-        total = jnp.zeros((hid, LANES), F32)
-        for n in range(chunks * LANES // wide):
-            columns = slice(n * wide, (n + 1) * wide)
-            pre = jnp.dot(w1_ref[...], xm_all[:, columns], preferred_element_type=F32)
-            left = jnp.maximum(pre[:, :LANES] + b1, 0.0)
-            right = jnp.maximum(pre[:, LANES:] + b1, 0.0)
-            if n == chunks * LANES // wide - 1:
-                h_seed = right
-                right = jnp.where(is_seed, 0.0, right)
-            total = total + left + right
-        g_mean = fold(total) * (1.0 / fan1)
+        for n in range(0, chunks - 2, 2):
+            left, right = layer(n)
+            summed = summed + left + right
+        left, h_seed = layer(chunks - 2)
+        summed = summed + left + jnp.where(is_seed, 0.0, h_seed)
+        g_mean = fold(summed) * (1.0 / fan1)
         stacked = jnp.concatenate([h_seed, g_mean], axis=0)
         z = jnp.zeros((hid, LANES), F32)
         for term in reversed(split_three(stacked)):

time: 19.7 us -> 19.5 us (0.990)
  Pallas kernels: 18.9 us -> 18.7 us
where the time goes in v6:
time: 19.5 us; the launch traced here: 19.3 us
  Pallas kernels  18.7 us (96%)
  local copies, waits for them, and re-layouts  0.63 us (3%)
    pallas_call x1, Pallas kernels, per_device(): pl.pallas_call(functools.partial(kernel, nd, nf), out_shape=pltpu.VMEM((h...  18.7 us
    unnamed x1, local copies, waits for them, and re-layouts  0.63 us

profile of v6, /device:TPU:0, one launch (start us, length us, event | category | flops | bytes accessed | tf_op | source)
XLA Modules:
  0.0 19.3 jit_solution(15719564956878594306)
XLA Ops:
  0.0 18.7 %shard_map.118 = f32[64,256]{1,0:T(8,128)S(1)} custom-call(bf16[32,16384]{1,0:T(8,128)(2,1)} %feat_hbm.1, s32[1,256]{1,0:T(1,128)} %bitcast.7, s32[1,8,128]{2,1,0:T(8,128)} %want_hbm.1, s32[1,8]{1,0:T(1,128)} %live_hbm.1, s32[15,256]{1,0:T(8,128)} %one_hbm.1, s32[10,15,256]{2,1,0:T(8,128)} %two_hbm.1, bf16[256,128]{1,0:T(8,128)(2,1)} %w1s_hbm.1, ...), custom_call_target="tpu_custom_call" | custom-call | tf_op jit(solution)/shard_map/pallas_call | solution.py:535
  18.7 0.6 %copy.14 = f32[64,256]{1,0:T(8,128)} copy(f32[64,256]{1,0:T(8,128)S(1)} %shard_map.118) | data formatting | bytes 131072
